TPU v7x, 256 devices: a whole 4x4x8 slice. The times are simulated.
256 devices in a mesh: dp: 32 (over y_hi, z, core), tp: 8 (over x, y_lo).
Axes of the slice: x: 4, y: 4 (y_hi: 2, y_lo: 2; y = y_hi * 2 + y_lo), z: 8, core: 2. Of those that a mesh axis runs over, the one named last changes fastest.
Arguments:
- hidden: bfloat16 [32768, 4096], P(('dp', 'tp')), may hold values from -24 to 24
- query_grad: bfloat16 [32768, 4096], P('dp', 'tp'), may hold values from -1.5 to 1.5
- key_grad: bfloat16 [32768, 1024], P('dp', 'tp'), may hold values from -1.5 to 1.5
- value_grad: bfloat16 [32768, 1024], P('dp', 'tp'), may hold values from -1.5 to 1.5
- w_query: bfloat16 [4096, 4096], P(None, 'tp'), may hold values from -0.09375 to 0.09375
- w_key: bfloat16 [4096, 1024], P(None, 'tp'), may hold values from -0.09375 to 0.09375
- w_value: bfloat16 [4096, 1024], P(None, 'tp'), may hold values from -0.09375 to 0.09375
Outputs:
- hidden_grad: bfloat16 [32768, 4096], P(('dp', 'tp'))
- grad_query: float32 [4096, 4096], P('dp', 'tp')
- grad_key: float32 [4096, 1024], P('dp', 'tp')
- grad_value: float32 [4096, 1024], P('dp', 'tp')
All inputs are finite; a program needn't handle non-finite values.
Results may differ from a plain program's by a relative error of at most 0.014.
Values may be sent and summed in bfloat16 or wider, within the bound.
No kernel may reach another device: no remote copies, remote signals or barrier semaphores. Data moves between devices by JAX's collectives and lax.ppermute only.
A program may use at most 256 MiB of HBM per device.

v0:
```python
import jax
import jax.numpy as jnp
from jax import lax
from jax.sharding import Mesh
from jax.sharding import PartitionSpec as P

TP = ("tp_0", "tp_1")
DP_TP = ("dp", "tp_0", "tp_1")


def scatter_axes(array, axes, dim):
    if not axes:
        return array
    nearer = lax.psum_scatter(array, axes[0], scatter_dimension=dim, tiled=True)
    return scatter_axes(nearer, axes[1:], dim)


def contract_rows(left, right):
    return lax.dot_general(
        left, right, (((0,), (0,)), ((), ())), preferred_element_type=jnp.float32
    )


def contract_cols(left, right):
    return lax.dot_general(
        left, right, (((1,), (1,)), ((), ())), preferred_element_type=jnp.float32
    )


def local(hidden, query_grad, key_grad, value_grad, w_query, w_key, w_value):
    query_width = w_query.shape[1]
    head_width = w_key.shape[1]
    all_grads = jnp.concatenate((query_grad, key_grad, value_grad), axis=1)
    all_weights = jnp.concatenate((w_query, w_key, w_value), axis=1)
    picked = all_grads
    total = contract_rows(lax.all_gather(hidden, TP, axis=0, tiled=True), picked)
    picked = all_grads
    summed = scatter_axes(contract_cols(picked, all_weights).astype(jnp.bfloat16), TP, 0).astype(
        jnp.float32
    )
    hidden_grad = summed.astype(jnp.bfloat16)
    weight_grad = lax.psum_scatter(
        total.astype(jnp.bfloat16), "dp", scatter_dimension=0, tiled=True
    ).astype(jnp.float32)
    grad_query = weight_grad[:, :query_width]
    grad_key = weight_grad[:, query_width : query_width + head_width]
    grad_value = weight_grad[:, query_width + head_width :]
    return (hidden_grad, grad_query, grad_key, grad_value)


def solution(mesh):
    torus = Mesh(mesh.devices.reshape(mesh.shape["dp"], 4, 2), ("dp", "tp_0", "tp_1"))
    in_specs = (
        P(DP_TP, None),
        P("dp", TP),
        P("dp", TP),
        P("dp", TP),
        P(None, TP),
        P(None, TP),
        P(None, TP),
    )
    out_specs = (P(DP_TP, None), P("dp", TP), P("dp", TP), P("dp", TP))
    return jax.shard_map(local, mesh=torus, in_specs=in_specs, out_specs=out_specs, check_vma=False)
```

profile of v0, /device:TPU:1, one launch (start us, length us, event | category | flops | bytes accessed | tf_op | source)
XLA Modules:
  0.0 389.5 jit_solution(8804540133229758166)
XLA Ops:
  8.0 0.0 all-gather.2.cloned.1.call-start
  8.0 0.7 all-gather.2.cloned.1.call-update
  8.7 0.0 reduce-scatter.6.cloned.1.call-start
  8.8 1.3 constant_dynamic-update-slice_fusion.2
  10.1 1.0 constant_dynamic-update-slice_fusion.1
  11.1 1.0 constant_dynamic-update-slice_fusion
  12.1 11.8 %convolution_convert_fusion = bf16[1024,4096]{1,0:T(8,128)(2,1)} fusion(bf16[1024,768]{1,0:T(8,128)(2,1)S(1)} %constant_dynamic-update-slice_fusion, bf16[4096,128]{1,0:T(8,128)(2,1)} %param.13, bf16[4096,128]{1,0:T(8,128)(2,1)} %param.12, bf16[4096,512]{1,0:T(8,128)(2,1)} %param.11), kind=kOutput, calls=%fused_computation | convolution fusion | flops 6465519616 | bytes 16252928 | tf_op jit(solution)/shard_map/dot_general | solution.py:25
  23.9 0.0 reduce-scatter.6.cloned.1.call-update
  23.9 0.0 reduce-scatter.10.cloned.1.call-start
  23.9 161.2 %all-gather.2.cloned.1.call-done = bf16[1024,4096]{1,0:T(8,128)(2,1)} async-done(((bf16[128,4096]{1,0:T(8,128)(2,1)}), bf16[1024,4096]{1,0:T(8,128)(2,1)}) %all-gather.2.cloned.1.call-update) | async-done | bytes 8388624 | tf_op jit(solution)/shard_map/all_gather | solution.py:36
  185.1 12.1 %fusion.5 = bf16[4096,768]{0,1:T(8,128)(2,1)} fusion(bf16[1024,768]{1,0:T(8,128)(2,1)S(1)} %constant_dynamic-update-slice_fusion, bf16[1024,4096]{1,0:T(8,128)(2,1)} %all-gather.2.cloned.1.call-done), kind=kOutput, calls=%fused_computation.7 | convolution fusion | flops 6445596672 | bytes 16252928 | tf_op jit(solution)/shard_map/dot_general | solution.py:19
  197.2 8.6 %copy.17 = bf16[4096,768]{1,0:T(8,128)(2,1)} copy(bf16[4096,768]{0,1:T(8,128)(2,1)} %fusion.5) | data formatting | bytes 12582912
  205.7 0.0 reduce-scatter.10.cloned.1.call-update
  205.8 0.0 reduce-scatter.8.cloned.1.call-start
  205.8 0.0 reduce-scatter.6.cloned.1.call-done
  205.8 0.5 reduce-scatter.8.cloned.1.call-update
  206.3 133.6 %reduce-scatter.10.cloned.1.call-done = bf16[128,768]{1,0:T(8,128)(2,1)} async-done(((bf16[4096,768]{1,0:T(8,128)(2,1)}), bf16[128,768]{1,0:T(8,128)(2,1)}) %reduce-scatter.10.cloned.1.call-update) | async-done | bytes 196624
  339.9 1.1 copy.18
  341.0 0.7 copy.16
  341.8 0.7 copy.15
  342.5 0.8 copy.14
  343.3 38.6 %reduce-scatter.8.cloned.1.call-done = bf16[128,4096]{1,0:T(8,128)(2,1)} async-done(((bf16[256,4096]{1,0:T(8,128)(2,1)}), bf16[128,4096]{1,0:T(8,128)(2,1)}) %reduce-scatter.8.cloned.1.call-update) | async-done | bytes 1048592 | tf_op jit(solution)/shard_map/reduce_scatter | solution.py:14
  (2 shorter events, 0.0 us)
Async XLA Ops:
  8.0 177.1 %all-gather.2.cloned.1.call-start = ((), (), s32[]{:S(2)}) async-start(), calls=%async_computation.5 | async-start | bytes 9437184 | tf_op jit(solution)/shard_map/all_gather | solution.py:36
  8.7 197.1 %reduce-scatter.6.cloned.1.call-start = ((), (), s32[]{:S(2)}) async-start(), calls=%async_computation.3 | async-start | bytes 10485760 | tf_op jit(solution)/shard_map/reduce_scatter | solution.py:14
  23.9 316.0 %reduce-scatter.10.cloned.1.call-start = ((), (), s32[]{:S(2)}) async-start(), calls=%async_computation.6 | async-start | bytes 6488064
  205.8 176.2 %reduce-scatter.8.cloned.1.call-start = ((), (), s32[]{:S(2)}) async-start(), calls=%async_computation.4 | async-start | bytes 3145728 | tf_op jit(solution)/shard_map/reduce_scatter | solution.py:14
Sparse Core Ops, SparseCore 0:
  10.6 174.4 all-gather.1
Sparse Core Ops, SparseCore 1:
  24.0 139.2 reduce-scatter.5
  205.8 134.0 reduce-scatter.9
  342.8 39.1 reduce-scatter.7
where the time goes:
time: 390 us
  waiting for transfers between devices  335 us (86%)
  matrix products  23.8 us (6%)
  between operations  15.7 us (4%)
  local copies, waits for them, and re-layouts  15.3 us (4%)
    all_gather x1, waiting for transfers between devices, local(): lax.all_gather(hidden, TP, axis=0, tiled=True)  161 us
    unnamed x5, waiting for transfers between devices  135 us
    reduce_scatter x2, waiting for transfers between devices, scatter_axes(): nearer = lax.psum_scatter(array, axes[0], scatter_dimension=dim, tiled=True)  38.6 us
    unnamed x7, local copies, waits for them, and re-layouts  14.3 us
    dot_general x1, matrix products, contract_rows(): lax.dot_general(left, right, (((0,), (0,)), ((), ())), preferred_element_...  12.1 us
    dot_general x1, matrix products, contract_cols(): lax.dot_general(left, right, (((1,), (1,)), ((), ())), preferred_element_...  11.8 us
  transfers between devices with their start and end apart: 4, of which 3 were waited for; matrix products, arithmetic and copies ran while one was open for 10% of the time, Pallas kernels for 0%

commit v1 on v0

v1 whole, which is shorter than its diff:
```python
import jax
import jax.numpy as jnp
from jax import lax
from jax.sharding import Mesh
from jax.sharding import PartitionSpec as P
from jax.experimental import pallas as pl
from jax.experimental.pallas import tpu as pltpu


AXES = ("yh", "z", "c", "x", "yl")
DP = ("yh", "z", "c")
TP = ("x", "yl")
BF16 = jnp.bfloat16
F32 = jnp.float32


def swap(value, axis, partner, size):
    return lax.ppermute(value, axis, [(i, partner(i)) for i in range(size)])


def flip(i):
    return i ^ 1


def sequential(**limits):
    return pltpu.CompilerParams(dimension_semantics=("arbitrary",), **limits)


def cut(index, weights, piece):
    widths = [w.shape[1] for w in weights]
    cols = sum(widths)

    def body(index, *refs):
        at = 0
        for ref, width in zip(refs[:-1], widths, strict=True):
            refs[-1][:, at : at + width] = ref[...]
            at += width

    return pl.pallas_call(
        body,
        name="cut",
        out_shape=jax.ShapeDtypeStruct((piece, cols), BF16),
        grid_spec=pltpu.PrefetchScalarGridSpec(
            num_scalar_prefetch=1,
            grid=(1,),
            in_specs=[pl.BlockSpec((piece, w), lambda i, t: (t[0], 0)) for w in widths],
            out_specs=pl.BlockSpec((piece, cols), lambda i, t: (0, 0)),
        ),
        compiler_params=sequential(),
    )(index, *weights)


def ordered(table, grads, tok):
    widths = [g.shape[1] for g in grads]
    cols = sum(widths)
    n_rows = grads[0].shape[0]
    steps = n_rows // tok

    def body(table, *refs):
        ins, outs = refs[:3], refs[3:]
        for i in range(2 * steps):
            row = pl.multiple_of(table[i] * tok, tok)
            at = 0
            for k, width in enumerate(widths):
                to = (i % steps) * tok
                outs[i // steps][to : to + tok, at : at + width] = ins[k][pl.ds(row, tok), :]
                at += width

    out = jax.ShapeDtypeStruct((n_rows, cols), BF16)
    return pl.pallas_call(
        body,
        name="ordered",
        out_shape=[out, out],
        grid_spec=pltpu.PrefetchScalarGridSpec(
            num_scalar_prefetch=1,
            grid=(1,),
            in_specs=[pl.BlockSpec(g.shape, lambda i, t: (0, 0)) for g in grads],
            out_specs=[pl.BlockSpec((n_rows, cols), lambda i, t: (0, 0))] * 2,
        ),
        compiler_params=sequential(),
    )(table, *grads)


def input_product(table, at, mine, got, weights, pieces, others):
    widths = [w.shape[1] for w in weights]
    cols = sum(widths)
    n_rows = mine.shape[0] // 2
    piece = pieces.shape[0] // 4
    steps = 4

    def body(table, mine, got, q, k, v, pieces, others, upper, lower):
        left = jnp.concatenate((q[...], k[...], v[...]), axis=1)
        south = table[2 * steps] == 0
        first = jnp.where(south, pieces[...], others[...])
        second = jnp.where(south, others[...], pieces[...])
        right = jnp.concatenate((first, second), axis=0)

        def times(a, b):
            return lax.dot_general(
                a[...], b, (((1,), (1,)), ((), ())), preferred_element_type=F32
            )

        total = (times(mine, left) + times(got, right)).astype(BF16)
        upper[...] = total[: n_rows // 2]
        lower[...] = total[n_rows // 2 :]

    row_spec = pl.BlockSpec((n_rows, cols), lambda i, t: (at, 0))
    piece_spec = pl.BlockSpec((piece, cols), lambda i, t: (t[steps + i], 0))
    return pl.pallas_call(
        body,
        out_shape=[jax.ShapeDtypeStruct((n_rows // 2, steps * 2 * piece), BF16)] * 2,
        grid_spec=pltpu.PrefetchScalarGridSpec(
            num_scalar_prefetch=1,
            grid=(steps,),
            in_specs=[row_spec, row_spec]
            + [pl.BlockSpec((2 * piece, w), lambda i, t: (t[i], 0)) for w in widths]
            + [piece_spec, piece_spec],
            out_specs=[pl.BlockSpec((n_rows // 2, 2 * piece), lambda i, t: (0, i))] * 2,
        ),
        compiler_params=sequential(),
        cost_estimate=pl.CostEstimate(
            flops=8 * n_rows * steps * piece * cols,
            bytes_accessed=8 * steps * piece * cols,
            transcendentals=0,
        ),
    )(table, mine, got, *weights, pieces, others)


def dot_rows(left, right):
    return lax.dot_general(left, right, (((0,), (0,)), ((), ())), preferred_element_type=F32)


def joined(arrays):
    return jnp.concatenate(arrays, axis=0)


def body(hidden, query_grad, key_grad, value_grad, w_query, w_key, w_value):
    n_x = lax.axis_size("x")
    n_z = lax.axis_size("z")
    yl = lax.axis_index("yl")
    yh = lax.axis_index("yh")
    x = lax.axis_index("x")
    c = lax.axis_index("c")
    z = lax.axis_index("z")
    tok, width = hidden.shape
    half = width // 2
    q_cols, k_cols = w_query.shape[1], w_key.shape[1]
    cols = q_cols + 2 * k_cols
    last = n_x - 1
    weights = (w_query, w_key, w_value)

    def near(i):
        return i ^ 1

    def far(i):
        return last - i

    def z_near(i):
        return i ^ 1

    def z_far(i):
        return (i - 1 + 2 * (i % 2)) % n_z

    own = lax.dynamic_slice(hidden, (0, yl * half), (tok, half))
    other = lax.dynamic_slice(hidden, (0, (1 - yl) * half), (tok, half))
    theirs = swap(other, "yl", flip, 2)
    piece = half // 8
    index = ((1 - yl) * 8 + 2 * (z % 4) + c)[None].astype(jnp.int32)
    part = swap(cut(index, weights, piece), "yl", flip, 2)
    x_near, x_far, x_both = x ^ 1, last - x, last - (x ^ 1)

    def order(mine):
        a, b = (yl, 1 - yl) if mine else (1 - yl, yl)
        near, far = 2 * jnp.stack((x_near, x_both)), 2 * jnp.stack((x_far, x_both))
        own_near, own_far = 2 * jnp.stack((x, x_near)), 2 * jnp.stack((x, x_far))
        return [far + a, near + b, own_near + a, own_far + b]

    table = jnp.concatenate(order(True) + order(False)).astype(jnp.int32)
    mine, sent = ordered(table, (query_grad, key_grad, value_grad), tok)
    got = swap(sent, "yl", flip, 2)

    def gather(block):
        to_near = swap(block, "x", near, n_x)
        to_far = swap(block, "x", far, n_x)
        upper = swap(to_far[: tok // 2], "x", near, n_x)
        lower = swap(to_near[tok // 2 :], "x", far, n_x)
        return to_near, to_far, upper, lower

    a_near, a_far, a_upper, a_lower = gather(own)
    b_near, b_far, b_upper, b_lower = gather(theirs)
    tokens = joined(
        (a_far, a_upper, a_lower, b_near, b_upper, b_lower, own, a_near, theirs, b_far)
    )

    z_one = swap(part, "z", z_near, n_z)
    z_two = swap(part, "z", z_far, n_z)
    low, high = z_two[: piece // 2], z_one[piece // 2 :]
    low = swap(low, "z", z_near, n_z)
    high = swap(high, "z", z_far, n_z)
    pieces = joined((part, z_one, z_two, low, high))
    others = swap(pieces, "c", flip, 2)
    where = [(z, z_near(z), z_far(z), z + 2)[k] % 4 for k in range(4)]
    block = jnp.arange(4)
    slot = sum(k * (block == where[k]) for k in range(4))
    table = jnp.concatenate((yl * 4 + block, slot, c[None])).astype(jnp.int32)

    def plus(left, right):
        return (left.astype(F32) + right.astype(F32)).astype(BF16)

    def weight_part(grad):
        total = dot_rows(tokens, grad).astype(BF16).reshape(n_z, 2, tok, cols)
        give = lax.dynamic_index_in_dim(total, 1 - c, 1, keepdims=False)
        return total, swap(give, "c", flip, 2)

    mine_total, come_mine = weight_part(mine)
    theirs_total, come_theirs = weight_part(got)

    n_w = n_z // 2
    w, parity = z // 2, z % 2

    def w_near(i):
        return i ^ 2

    def w_far(i):
        return (i - 2 + 4 * (i // 2 % 2)) % n_z

    def ring(total, come, first):
        total = total.reshape(n_w, 2, 2, tok, cols)
        come = come.reshape(n_w, 2, tok, cols)

        def chunks(at, count, side):
            mine = lax.dynamic_slice(total, (at, side, c, 0, 0), (count, 1, 1, tok, cols))
            other = lax.dynamic_slice(come, (at, side, 0, 0), (count, 1, tok, cols))
            return mine[:, 0, 0].astype(F32) + other[:, 0].astype(F32)

        given = chunks(0, n_w, 1 - parity).astype(BF16)
        near = swap(given, "z", z_far if first else z_near, n_z)

        def chunk(step):
            forward = (w + step + first) % 2 == 0
            left = n_w - 1 - step
            to = jnp.where(forward, w + left, w - left + n_w) % n_w
            return chunks(to, 1, parity)[0] + lax.dynamic_index_in_dim(
                near, to, 0, keepdims=False
            ).astype(F32)

        passed = chunk(0).astype(BF16)
        for step in range(1, n_w):
            side = w_near if (step + first) % 2 else w_far
            taken = swap(passed, "z", side, n_z)
            passed = (taken.astype(F32) + chunk(step)).astype(BF16)
        return passed

    part_mine = ring(mine_total, come_mine, 0)
    part_theirs = ring(theirs_total, come_theirs, 1)

    args = (mine, got, weights, pieces, others)
    a_send, b_send = input_product(table, 0, *args)
    a_keep, b_keep = input_product(table, 1, *args)

    def pair_sum(keep, send, one, two):
        taken = swap(send, "x", one, n_x)
        mine, given = plus(keep[:tok], taken[:tok]), plus(keep[tok:], taken[tok:])
        taken = swap(given, "x", two, n_x)
        return plus(mine, taken)

    b_sum = pair_sum(b_keep, b_send, near, far)
    a_sum = pair_sum(a_keep, a_send, far, near)
    a_other = swap(b_sum, "yl", flip, 2)
    hidden_grad = jnp.where(
        yl == 0,
        jnp.concatenate((a_sum, a_other), axis=1),
        jnp.concatenate((a_other, a_sum), axis=1),
    )

    same = yh == yl
    first = jnp.where(same, part_mine, part_theirs)
    second = jnp.where(same, part_theirs, part_mine)
    home = [(2 * a + b, 2 * b + a) for a in range(2) for b in range(2)]
    away = [(2 * a + b, 2 * b + 1 - a) for a in range(2) for b in range(2)]
    first = lax.ppermute(first, ("yh", "yl"), home)
    second = lax.ppermute(second, ("yh", "yl"), away)
    weight_grad = first.astype(F32) + second.astype(F32)
    return (
        hidden_grad,
        weight_grad[:, :q_cols],
        weight_grad[:, q_cols : q_cols + k_cols],
        weight_grad[:, q_cols + k_cols :],
    )


def solution(mesh):
    torus = Mesh(mesh.devices.reshape(2, 8, 2, 4, 2), AXES)
    in_specs = (P(AXES, None),) + (P(DP, TP),) * 3 + (P(None, TP),) * 3
    out_specs = (P(AXES, None),) + (P(DP, TP),) * 3
    return jax.shard_map(body, mesh=torus, in_specs=in_specs, out_specs=out_specs, check_vma=False)
```

time: 390 us -> 188 us (0.48)
  the two profiles are of different devices: /device:TPU:1 before, /device:TPU:46 now
where the time goes in v1:
time: 188 us; the launch traced here: 187 us
  waiting for transfers between devices  76.8 us (41%)
  starting transfers between devices  48.6 us (26%)
  Pallas kernels  22.4 us (12%)
  other arithmetic  19.1 us (10%)
  local copies, waits for them, and re-layouts  9.97 us (5%)
  matrix products  9.06 us (5%)
    ppermute x31, waiting for transfers between devices, swap(): return lax.ppermute(value, axis, [(i, partner(i)) for i in range(size)])  72.4 us
    ppermute x31, starting transfers between devices, swap(): return lax.ppermute(value, axis, [(i, partner(i)) for i in range(size)])  44.3 us
    pallas_call x2, Pallas kernels, input_product(): pl.pallas_call(body, out_shape=[jax.ShapeDtypeStruct((n_rows // 2, steps...  16.6 us
    dot_general x2, matrix products, dot_rows(): lax.dot_general(left, right, (((0,), (0,)), ((), ())), preferred_element_...  9.06 us
    convert_element_type x4, other arithmetic, plus(): return (left.astype(F32) + right.astype(F32)).astype(BF16)  4.89 us
    convert_element_type x4, other arithmetic, ring(): passed = (taken.astype(F32) + chunk(step)).astype(BF16)  4.49 us
    ppermute x1, waiting for transfers between devices, body(): first = lax.ppermute(first, ('yh', 'yl'), home)  4.18 us
    pallas_call x1, Pallas kernels, ordered(): pl.pallas_call(body, name='ordered', out_shape=[out, out], grid_spec=pltp...  4.02 us
  transfers between devices with their start and end apart: 33, of which 16 were waited for; matrix products, arithmetic and copies ran while one was open for 18% of the time, Pallas kernels for 12%

profile of v1, /device:TPU:46, one launch (start us, length us, event | category | flops | bytes accessed | tf_op | source)
XLA Modules:
  0.0 187.0 jit_solution(17581015930393042714)
XLA Ops:
  0.6 2.1 %constant_dynamic-slice_fusion = (bf16[128,2048]{1,0:T(8,128)(2,1)}, bf16[128,2048]{1,0:T(8,128)(2,1)S(1)}) fusion(bf16[128,4096]{1,0:T(8,128)(2,1)} %param.7, s32[]{:T(128)S(6)} %select_n.225, s32[]{:T(128)S(6)} %select_n.224), kind=kLoop, calls=%fused_computation.63 | loop fusion | bytes 2097160 | tf_op jit(solution)/shard_map/dynamic_slice | solution.py:165
  8.8 4.0 %ordered.1 = (bf16[1024,768]{1,0:T(8,128)(2,1)}, bf16[1024,768]{1,0:T(8,128)(2,1)}) custom-call(s32[16]{0:T(128)} %concatenate.19.table, bf16[1024,512]{1,0:T(8,128)(2,1)} %refs_0_.2, bf16[1024,128]{1,0:T(8,128)(2,1)} %refs_1_.2, bf16[1024,128]{1,0:T(8,128)(2,1)} %refs_2_.2), custom_call_target="tpu_custom_call" | custom-call | tf_op jit(solution)/shard_map/ordered/pallas_call | solution.py:70
  13.3 4.3 %collective-permute-done.12 = bf16[128,2048]{1,0:T(8,128)(2,1)S(1)} collective-permute-done((bf16[128,2048]{1,0:T(8,128)(2,1)S(1)}, bf16[128,2048]{1,0:T(8,128)(2,1)S(1)}, u32[]{:S(2)}, u32[]{:S(2)}) %collective-permute-start.12) | collective-permute-done | bytes 524320 | tf_op jit(solution)/shard_map/ppermute | solution.py:18
  18.3 2.2 %collective-permute-start.15 = (bf16[64,2048]{1,0:T(8,128)(2,1)S(1)}, bf16[64,2048]{1,0:T(8,128)(2,1)S(1)}, u32[]{:S(2)}, u32[]{:S(2)}) collective-permute-start(bf16[64,2048]{1,0:T(8,128)(2,1)S(1)} %slice.75), channel_id=1, source_target_pairs={{0,6},{2,4},{4,2},{6,0},{1,7},{3,5},{5,3},{7,1},{8,14},{10,12},{12... | collective-permute-start | bytes 786440 | tf_op jit(solution)/shard_map/ppermute | solution.py:18
  20.6 8.9 %collective-permute-done.16 = bf16[128,2048]{1,0:T(8,128)(2,1)} collective-permute-done((bf16[128,2048]{1,0:T(8,128)(2,1)}, bf16[128,2048]{1,0:T(8,128)(2,1)}, u32[]{:S(2)}, u32[]{:S(2)}) %collective-permute-start.16) | collective-permute-done | bytes 524320 | tf_op jit(solution)/shard_map/ppermute | solution.py:18
  29.4 1.9 %collective-permute-start.3 = (bf16[256,768]{1,0:T(8,128)(2,1)S(1)}, bf16[256,768]{1,0:T(8,128)(2,1)S(1)}, u32[]{:S(2)}, u32[]{:S(2)}) collective-permute-start(bf16[256,768]{1,0:T(8,128)(2,1)S(1)} %collective-permute-done.1), channel_id=1, source_target_pairs={{0,112},{16,32},{32,16},{48,64},{64,48},{80,96},{96,80},{112,0},{1... | collective-permute-start | bytes 1179656 | tf_op jit(solution)/shard_map/ppermute | solution.py:18
  32.5 2.8 %collective-permute-start.18 = (bf16[128,2048]{1,0:T(8,128)(2,1)}, bf16[128,2048]{1,0:T(8,128)(2,1)S(1)}, u32[]{:S(2)}, u32[]{:S(2)}) collective-permute-start(bf16[128,2048]{1,0:T(8,128)(2,1)} %collective-permute-done.16), channel_id=1, source_target_pairs={{0,6},{2,4},{4,2},{6,0},{1,7},{3,5},{5,3},{7,1},{8,14},{10,12},{12... | collective-permute-start | bytes 1572872 | tf_op jit(solution)/shard_map/ppermute | solution.py:18
  35.4 1.9 %collective-permute-done.3 = bf16[256,768]{1,0:T(8,128)(2,1)S(1)} collective-permute-done((bf16[256,768]{1,0:T(8,128)(2,1)S(1)}, bf16[256,768]{1,0:T(8,128)(2,1)S(1)}, u32[]{:S(2)}, u32[]{:S(2)}) %collective-permute-start.3) | collective-permute-done | bytes 393248 | tf_op jit(solution)/shard_map/ppermute | solution.py:18
  37.4 4.1 %collective-permute-start.4 = (bf16[128,768]{1,0:T(8,128)(2,1)S(1)}, bf16[128,768]{1,0:T(8,128)(2,1)S(1)}, u32[]{:S(2)}, u32[]{:S(2)}) collective-permute-start(bf16[128,768]{1,0:T(8,128)(2,1)S(1)} %slice.68), channel_id=1, source_target_pairs={{0,16},{16,0},{32,48},{48,32},{64,80},{80,64},{96,112},{112,96},{1... | collective-permute-start | bytes 589832 | tf_op jit(solution)/shard_map/ppermute | solution.py:18
  42.7 2.5 %collective-permute-done.4 = bf16[128,768]{1,0:T(8,128)(2,1)S(1)} collective-permute-done((bf16[128,768]{1,0:T(8,128)(2,1)S(1)}, bf16[128,768]{1,0:T(8,128)(2,1)S(1)}, u32[]{:S(2)}, u32[]{:S(2)}) %collective-permute-start.4) | collective-permute-done | bytes 196640 | tf_op jit(solution)/shard_map/ppermute | solution.py:18
  47.5 2.5 %collective-permute-start.20 = (bf16[64,2048]{1,0:T(8,128)(2,1)S(1)}, bf16[64,2048]{1,0:T(8,128)(2,1)S(1)}, u32[]{:S(2)}, u32[]{:S(2)}) collective-permute-start(bf16[64,2048]{1,0:T(8,128)(2,1)S(1)} %slice.77), channel_id=1, source_target_pairs={{0,6},{2,4},{4,2},{6,0},{1,7},{3,5},{5,3},{7,1},{8,14},{10,12},{12... | collective-permute-start | bytes 786440 | tf_op jit(solution)/shard_map/ppermute | solution.py:18
  51.7 6.0 %collective-permute-done.20 = bf16[64,2048]{1,0:T(8,128)(2,1)S(1)} collective-permute-done((bf16[64,2048]{1,0:T(8,128)(2,1)S(1)}, bf16[64,2048]{1,0:T(8,128)(2,1)S(1)}, u32[]{:S(2)}, u32[]{:S(2)}) %collective-permute-start.20) | collective-permute-done | bytes 262176 | tf_op jit(solution)/shard_map/ppermute | solution.py:18
  58.9 3.7 %convolution_convert_fusion.1 = bf16[2048,768]{1,0:T(8,128)(2,1)S(1)} fusion(bf16[1024,2048]{1,0:T(8,128)(2,1)S(1)} %constant_dynamic-update-slice_fusion.5, bf16[1024,768]{1,0:T(8,128)(2,1)S(1)} %copy-done.1), kind=kOutput, calls=%fused_computation.1 | convolution fusion | flops 3222798336 | bytes 8912896 | tf_op jit(solution)/shard_map/dot_general | solution.py:130
  64.1 5.3 %convolution_convert_fusion = bf16[2048,768]{1,0:T(8,128)(2,1)S(1)} fusion(bf16[1024,2048]{1,0:T(8,128)(2,1)S(1)} %constant_dynamic-update-slice_fusion.5, bf16[1024,768]{1,0:T(8,128)(2,1)} %collective-permute-done.got), kind=kOutput, calls=%fused_computation | convolution fusion | flops 3222798336 | bytes 8912896 | tf_op jit(solution)/shard_map/dot_general | solution.py:130
  73.3 8.5 %shard_map.103 = (bf16[256,2048]{1,0:T(8,128)(2,1)}, bf16[256,2048]{1,0:T(8,128)(2,1)}) custom-call(s32[9]{0:T(128)} %pad_add_fusion.table, bf16[1024,768]{1,0:T(8,128)(2,1)} %get-tuple-element.10.mine, bf16[1024,768]{1,0:T(8,128)(2,1)} %collective-permute-done.got, bf16[4096,512]{1,0:T(8,128)(2,1)} %q.3, bf16[4096,128]{1,0:T(8,128)(2,1)} %k.3, ...), custom_call_target="tpu_custom_call" | custom-call | flops 3221225472 | bytes 6291456 | tf_op jit(solution)/shard_map/pallas_call | solution.py:109
  82.1 2.2 %fusion.1 = bf16[4,128,768]{2,1,0:T(8,128)(2,1)} fusion(bf16[4,2,128,768]{3,2,1,0:T(8,128)(2,1)} %bitcast.10, s32[]{:T(128)S(6)} %select_n.234, bf16[4,2,2,128,768]{4,3,2,1,0:T(8,128)(2,1)S(1)} %bitcast.115, s32[]{:T(128)S(6)} %select_n.232), kind=kLoop, calls=%fused_computation.5 | loop fusion | flops 1572864 | bytes 2359304 | tf_op jit(solution)/shard_map/convert_element_type | solution.py:236
  84.3 1.8 collective-permute-start.22
  86.2 2.3 %collective-permute-start.7 = (bf16[256,2048]{1,0:T(8,128)(2,1)}, bf16[256,2048]{1,0:T(8,128)(2,1)}, u32[]{:S(2)}, u32[]{:S(2)}) collective-permute-start(bf16[256,2048]{1,0:T(8,128)(2,1)} %get-tuple-element.13), channel_id=1, source_target_pairs={{0,6},{2,4},{4,2},{6,0},{1,7},{3,5},{5,3},{7,1},{8,14},{10,12},{12... | collective-permute-start | bytes 3145736 | tf_op jit(solution)/shard_map/ppermute | solution.py:18
  88.5 8.1 %shard_map.102 = (bf16[256,2048]{1,0:T(8,128)(2,1)}, bf16[256,2048]{1,0:T(8,128)(2,1)}) custom-call(s32[9]{0:T(128)} %pad_add_fusion.table, bf16[1024,768]{1,0:T(8,128)(2,1)} %get-tuple-element.10.mine, bf16[1024,768]{1,0:T(8,128)(2,1)} %collective-permute-done.got, bf16[4096,512]{1,0:T(8,128)(2,1)} %q.3, bf16[4096,128]{1,0:T(8,128)(2,1)} %k.3, ...), custom_call_target="tpu_custom_call" | custom-call | flops 3221225472 | bytes 6291456 | tf_op jit(solution)/shard_map/pallas_call | solution.py:109
  99.4 4.6 %collective-permute-done.22 = bf16[4,128,768]{2,1,0:T(8,128)(2,1)} collective-permute-done((bf16[4,128,768]{2,1,0:T(8,128)(2,1)}, bf16[4,128,768]{2,1,0:T(8,128)(2,1)}, u32[]{:S(2)}, u32[]{:S(2)}) %collective-permute-start.22) | collective-permute-done | bytes 786464 | tf_op jit(solution)/shard_map/ppermute | solution.py:18
  105.2 2.3 %collective-permute-start.23 = (bf16[128,768]{1,0:T(8,128)(2,1)S(1)}, bf16[128,768]{1,0:T(8,128)(2,1)S(1)}, u32[]{:S(2)}, u32[]{:S(2)}) collective-permute-start(bf16[128,768]{1,0:T(8,128)(2,1)S(1)} %fusion.15), channel_id=1, source_target_pairs={{0,32},{16,48},{32,0},{48,16},{64,96},{80,112},{96,64},{112,80},{1... | collective-permute-start | bytes 589832 | tf_op jit(solution)/shard_map/ppermute | solution.py:18
  108.6 2.4 %collective-permute-start.10 = (bf16[128,2048]{1,0:T(8,128)(2,1)S(1)}, bf16[128,2048]{1,0:T(8,128)(2,1)S(1)}, u32[]{:S(2)}, u32[]{:S(2)}) collective-permute-start(bf16[128,2048]{1,0:T(8,128)(2,1)S(1)} %add_convert_fusion.1), channel_id=1, source_target_pairs={{0,6},{2,4},{4,2},{6,0},{1,7},{3,5},{5,3},{7,1},{8,14},{10,12},{12... | collective-permute-start | bytes 1572872 | tf_op jit(solution)/shard_map/ppermute | solution.py:18
  111.0 13.1 %collective-permute-done.23 = bf16[128,768]{1,0:T(8,128)(2,1)S(1)} collective-permute-done((bf16[128,768]{1,0:T(8,128)(2,1)S(1)}, bf16[128,768]{1,0:T(8,128)(2,1)S(1)}, u32[]{:S(2)}, u32[]{:S(2)}) %collective-permute-start.23) | collective-permute-done | bytes 196640 | tf_op jit(solution)/shard_map/ppermute | solution.py:18
  125.2 5.7 %collective-permute-start.24 = (bf16[128,768]{1,0:T(8,128)(2,1)S(1)}, bf16[128,768]{1,0:T(8,128)(2,1)S(1)}, u32[]{:S(2)}, u32[]{:S(2)}) collective-permute-start(bf16[128,768]{1,0:T(8,128)(2,1)S(1)} %fusion.14), channel_id=1, source_target_pairs={{0,96},{16,112},{32,64},{48,80},{64,32},{80,48},{96,0},{112,16},{1... | collective-permute-start | bytes 589832 | tf_op jit(solution)/shard_map/ppermute | solution.py:18
  134.7 8.9 %collective-permute-done.24 = bf16[128,768]{1,0:T(8,128)(2,1)S(1)} collective-permute-done((bf16[128,768]{1,0:T(8,128)(2,1)S(1)}, bf16[128,768]{1,0:T(8,128)(2,1)S(1)}, u32[]{:S(2)}, u32[]{:S(2)}) %collective-permute-start.24) | collective-permute-done | bytes 196640 | tf_op jit(solution)/shard_map/ppermute | solution.py:18
  145.1 2.2 %collective-permute-done.28 = bf16[128,768]{1,0:T(8,128)(2,1)S(1)} collective-permute-done((bf16[128,768]{1,0:T(8,128)(2,1)S(1)}, bf16[128,768]{1,0:T(8,128)(2,1)S(1)}, u32[]{:S(2)}, u32[]{:S(2)}) %collective-permute-start.28) | collective-permute-done | bytes 196640 | tf_op jit(solution)/shard_map/ppermute | solution.py:18
  150.8 10.4 %collective-permute-done.29 = bf16[128,768]{1,0:T(8,128)(2,1)S(1)} collective-permute-done((bf16[128,768]{1,0:T(8,128)(2,1)S(1)}, bf16[128,768]{1,0:T(8,128)(2,1)S(1)}, u32[]{:S(2)}, u32[]{:S(2)}) %collective-permute-start.29) | collective-permute-done | bytes 196640 | tf_op jit(solution)/shard_map/ppermute | solution.py:18
  162.3 3.9 %collective-permute-start.30 = (bf16[128,768]{1,0:T(8,128)(2,1)S(1)}, bf16[128,768]{1,0:T(8,128)(2,1)S(1)}, u32[]{:S(2)}, u32[]{:S(2)}) collective-permute-start(bf16[128,768]{1,0:T(8,128)(2,1)S(1)} %fusion.5), channel_id=1, source_target_pairs={{0,96},{16,112},{32,64},{48,80},{64,32},{80,48},{96,0},{112,16},{1... | collective-permute-start | bytes 589832 | tf_op jit(solution)/shard_map/ppermute | solution.py:18
  167.6 6.6 %collective-permute-done.30 = bf16[128,768]{1,0:T(8,128)(2,1)S(1)} collective-permute-done((bf16[128,768]{1,0:T(8,128)(2,1)S(1)}, bf16[128,768]{1,0:T(8,128)(2,1)S(1)}, u32[]{:S(2)}, u32[]{:S(2)}) %collective-permute-start.30) | collective-permute-done | bytes 196640 | tf_op jit(solution)/shard_map/ppermute | solution.py:18
  175.7 2.4 %collective-permute-start.32 = (bf16[128,768]{1,0:T(8,128)(2,1)S(1)}, bf16[128,768]{1,0:T(8,128)(2,1)S(1)}, u32[]{:S(2)}, u32[]{:S(2)}) collective-permute-start(bf16[128,768]{1,0:T(8,128)(2,1)S(1)} %broadcast_select_fusion), channel_id=1, source_target_pairs={{0,1},{1,129},{128,0},{129,128},{2,3},{3,131},{130,2},{131,130},{4... | collective-permute-start | bytes 589832 | tf_op jit(solution)/shard_map/ppermute | solution.py:282
  178.0 1.9 %collective-permute-start.31 = (bf16[128,768]{1,0:T(8,128)(2,1)S(1)}, bf16[128,768]{1,0:T(8,128)(2,1)S(1)}, u32[]{:S(2)}, u32[]{:S(2)}) collective-permute-start(bf16[128,768]{1,0:T(8,128)(2,1)S(1)} %get-tuple-element.16), channel_id=1, source_target_pairs={{0,0},{1,128},{128,1},{129,129},{2,2},{3,130},{130,3},{131,131},{4... | collective-permute-start | bytes 589832 | tf_op jit(solution)/shard_map/ppermute | solution.py:281
  181.4 4.2 %collective-permute-done.31 = bf16[128,768]{1,0:T(8,128)(2,1)S(1)} collective-permute-done((bf16[128,768]{1,0:T(8,128)(2,1)S(1)}, bf16[128,768]{1,0:T(8,128)(2,1)S(1)}, u32[]{:S(2)}, u32[]{:S(2)}) %collective-permute-start.31) | collective-permute-done | bytes 196640 | tf_op jit(solution)/shard_map/ppermute | solution.py:281
  (112 shorter events, 42.0 us)
Async XLA Ops:
  2.7 14.9 %collective-permute-start.12 = (bf16[128,2048]{1,0:T(8,128)(2,1)S(1)}, bf16[128,2048]{1,0:T(8,128)(2,1)S(1)}, u32[]{:S(2)}, u32[]{:S(2)}) collective-permute-start(bf16[128,2048]{1,0:T(8,128)(2,1)S(1)} %get-tuple-element.20), channel_id=1, source_target_pairs={{0,6},{2,4},{4,2},{6,0},{1,7},{3,5},{5,3},{7,1},{8,14},{10,12},{12... | collective-permute-start | bytes 1572872 | tf_op jit(solution)/shard_map/ppermute | solution.py:18
  3.2 15.1 %collective-permute-start.14 = (bf16[128,2048]{1,0:T(8,128)(2,1)S(1)}, bf16[128,2048]{1,0:T(8,128)(2,1)S(1)}, u32[]{:S(2)}, u32[]{:S(2)}) collective-permute-start(bf16[128,2048]{1,0:T(8,128)(2,1)S(1)} %get-tuple-element.20), channel_id=1, source_target_pairs={{0,2},{2,0},{4,6},{6,4},{1,3},{3,1},{5,7},{7,5},{8,10},{10,8},{12,... | collective-permute-start | bytes 1572872 | tf_op jit(solution)/shard_map/ppermute | solution.py:18
  5.9 12.2 %collective-permute-start.1 = (bf16[256,768]{1,0:T(8,128)(2,1)}, bf16[256,768]{1,0:T(8,128)(2,1)S(1)}, u32[]{:S(2)}, u32[]{:S(2)}) collective-permute-start(bf16[256,768]{1,0:T(8,128)(2,1)} %cut.1), channel_id=1, source_target_pairs={{0,1},{1,0},{2,3},{3,2},{4,5},{5,4},{6,7},{7,6},{8,9},{9,8},{10,11... | collective-permute-start | bytes 1179656 | tf_op jit(solution)/shard_map/ppermute | solution.py:18
  6.3 23.1 %collective-permute-start.16 = (bf16[128,2048]{1,0:T(8,128)(2,1)}, bf16[128,2048]{1,0:T(8,128)(2,1)}, u32[]{:S(2)}, u32[]{:S(2)}) collective-permute-start(bf16[128,2048]{1,0:T(8,128)(2,1)} %get-tuple-element.19), channel_id=1, source_target_pairs={{0,1},{1,0},{2,3},{3,2},{4,5},{5,4},{6,7},{7,6},{8,9},{9,8},{10,11... | collective-permute-start | bytes 1572872 | tf_op jit(solution)/shard_map/ppermute | solution.py:18
  12.9 51.2 %collective-permute-start = (bf16[1024,768]{1,0:T(8,128)(2,1)}, bf16[1024,768]{1,0:T(8,128)(2,1)}, u32[]{:S(2)}, u32[]{:S(2)}) collective-permute-start(bf16[1024,768]{1,0:T(8,128)(2,1)} %get-tuple-element.11), channel_id=1, source_target_pairs={{0,1},{1,0},{2,3},{3,2},{4,5},{5,4},{6,7},{7,6},{8,9},{9,8},{10,11... | collective-permute-start | bytes 4718600 | tf_op jit(solution)/shard_map/ppermute | solution.py:18
  17.6 13.7 %collective-permute-start.13 = (bf16[64,2048]{1,0:T(8,128)(2,1)S(1)}, bf16[64,2048]{1,0:T(8,128)(2,1)S(1)}, u32[]{:S(2)}, u32[]{:S(2)}) collective-permute-start(bf16[64,2048]{1,0:T(8,128)(2,1)S(1)} %slice.74), channel_id=1, source_target_pairs={{0,2},{2,0},{4,6},{6,4},{1,3},{3,1},{5,7},{7,5},{8,10},{10,8},{12,... | collective-permute-start | bytes 786440 | tf_op jit(solution)/shard_map/ppermute | solution.py:18
  18.1 23.4 %collective-permute-start.2 = (bf16[256,768]{1,0:T(8,128)(2,1)S(1)}, bf16[256,768]{1,0:T(8,128)(2,1)S(1)}, u32[]{:S(2)}, u32[]{:S(2)}) collective-permute-start(bf16[256,768]{1,0:T(8,128)(2,1)S(1)} %collective-permute-done.1), channel_id=1, source_target_pairs={{0,16},{16,0},{32,48},{48,32},{64,80},{80,64},{96,112},{112,96},{1... | collective-permute-start | bytes 1179656 | tf_op jit(solution)/shard_map/ppermute | solution.py:18
  18.3 14.2 %collective-permute-start.15 = (bf16[64,2048]{1,0:T(8,128)(2,1)S(1)}, bf16[64,2048]{1,0:T(8,128)(2,1)S(1)}, u32[]{:S(2)}, u32[]{:S(2)}) collective-permute-start(bf16[64,2048]{1,0:T(8,128)(2,1)S(1)} %slice.75), channel_id=1, source_target_pairs={{0,6},{2,4},{4,2},{6,0},{1,7},{3,5},{5,3},{7,1},{8,14},{10,12},{12... | collective-permute-start | bytes 786440 | tf_op jit(solution)/shard_map/ppermute | solution.py:18
  29.4 7.9 %collective-permute-start.3 = (bf16[256,768]{1,0:T(8,128)(2,1)S(1)}, bf16[256,768]{1,0:T(8,128)(2,1)S(1)}, u32[]{:S(2)}, u32[]{:S(2)}) collective-permute-start(bf16[256,768]{1,0:T(8,128)(2,1)S(1)} %collective-permute-done.1), channel_id=1, source_target_pairs={{0,112},{16,32},{32,16},{48,64},{64,48},{80,96},{96,80},{112,0},{1... | collective-permute-start | bytes 1179656 | tf_op jit(solution)/shard_map/ppermute | solution.py:18
  31.4 16.1 %collective-permute-start.17 = (bf16[128,2048]{1,0:T(8,128)(2,1)}, bf16[128,2048]{1,0:T(8,128)(2,1)S(1)}, u32[]{:S(2)}, u32[]{:S(2)}) collective-permute-start(bf16[128,2048]{1,0:T(8,128)(2,1)} %collective-permute-done.16), channel_id=1, source_target_pairs={{0,2},{2,0},{4,6},{6,4},{1,3},{3,1},{5,7},{7,5},{8,10},{10,8},{12,... | collective-permute-start | bytes 1572872 | tf_op jit(solution)/shard_map/ppermute | solution.py:18
  32.5 12.6 %collective-permute-start.18 = (bf16[128,2048]{1,0:T(8,128)(2,1)}, bf16[128,2048]{1,0:T(8,128)(2,1)S(1)}, u32[]{:S(2)}, u32[]{:S(2)}) collective-permute-start(bf16[128,2048]{1,0:T(8,128)(2,1)} %collective-permute-done.16), channel_id=1, source_target_pairs={{0,6},{2,4},{4,2},{6,0},{1,7},{3,5},{5,3},{7,1},{8,14},{10,12},{12... | collective-permute-start | bytes 1572872 | tf_op jit(solution)/shard_map/ppermute | solution.py:18
  37.4 7.8 %collective-permute-start.4 = (bf16[128,768]{1,0:T(8,128)(2,1)S(1)}, bf16[128,768]{1,0:T(8,128)(2,1)S(1)}, u32[]{:S(2)}, u32[]{:S(2)}) collective-permute-start(bf16[128,768]{1,0:T(8,128)(2,1)S(1)} %slice.68), channel_id=1, source_target_pairs={{0,16},{16,0},{32,48},{48,32},{64,80},{80,64},{96,112},{112,96},{1... | collective-permute-start | bytes 589832 | tf_op jit(solution)/shard_map/ppermute | solution.py:18
  41.5 5.8 %collective-permute-start.5 = (bf16[128,768]{1,0:T(8,128)(2,1)S(1)}, bf16[128,768]{1,0:T(8,128)(2,1)S(1)}, u32[]{:S(2)}, u32[]{:S(2)}) collective-permute-start(bf16[128,768]{1,0:T(8,128)(2,1)S(1)} %slice.69), channel_id=1, source_target_pairs={{0,112},{16,32},{32,16},{48,64},{64,48},{80,96},{96,80},{112,0},{1... | collective-permute-start | bytes 589832 | tf_op jit(solution)/shard_map/ppermute | solution.py:18
  45.2 6.5 %collective-permute-start.19 = (bf16[64,2048]{1,0:T(8,128)(2,1)S(1)}, bf16[64,2048]{1,0:T(8,128)(2,1)S(1)}, u32[]{:S(2)}, u32[]{:S(2)}) collective-permute-start(bf16[64,2048]{1,0:T(8,128)(2,1)S(1)} %slice.76), channel_id=1, source_target_pairs={{0,2},{2,0},{4,6},{6,4},{1,3},{3,1},{5,7},{7,5},{8,10},{10,8},{12,... | collective-permute-start | bytes 786440 | tf_op jit(solution)/shard_map/ppermute | solution.py:18
  47.3 26.0 %collective-permute-start.6 = (bf16[1024,768]{1,0:T(8,128)(2,1)S(1)}, bf16[1024,768]{1,0:T(8,128)(2,1)}, u32[]{:S(2)}, u32[]{:S(2)}) collective-permute-start(bf16[1024,768]{1,0:T(8,128)(2,1)S(1)} %constant_dynamic-update-slice_fusion.pieces), channel_id=1, source_target_pairs={{0,8},{8,0},{1,9},{9,1},{2,10},{10,2},{3,11},{11,3},{4,12},{12,4},... | collective-permute-start | bytes 4718600 | tf_op jit(solution)/shard_map/ppermute | solution.py:18
  47.5 10.2 %collective-permute-start.20 = (bf16[64,2048]{1,0:T(8,128)(2,1)S(1)}, bf16[64,2048]{1,0:T(8,128)(2,1)S(1)}, u32[]{:S(2)}, u32[]{:S(2)}) collective-permute-start(bf16[64,2048]{1,0:T(8,128)(2,1)S(1)} %slice.77), channel_id=1, source_target_pairs={{0,6},{2,4},{4,2},{6,0},{1,7},{3,5},{5,3},{7,1},{8,14},{10,12},{12... | collective-permute-start | bytes 786440 | tf_op jit(solution)/shard_map/ppermute | solution.py:18
  64.1 18.0 %collective-permute-start.21 = (bf16[8,128,768]{2,1,0:T(8,128)(2,1)}, bf16[8,128,768]{2,1,0:T(8,128)(2,1)}, u32[]{:S(2)}, u32[]{:S(2)}) collective-permute-start(bf16[8,128,768]{2,1,0:T(8,128)(2,1)} %dynamic-slice_bitcast_fusion.1), channel_id=1, source_target_pairs={{0,8},{8,0},{1,9},{9,1},{2,10},{10,2},{3,11},{11,3},{4,12},{12,4},... | collective-permute-start | bytes 4718600 | tf_op jit(solution)/shard_map/ppermute | solution.py:18
  72.3 24.3 %collective-permute-start.26 = (bf16[8,128,768]{2,1,0:T(8,128)(2,1)}, bf16[8,128,768]{2,1,0:T(8,128)(2,1)}, u32[]{:S(2)}, u32[]{:S(2)}) collective-permute-start(bf16[8,128,768]{2,1,0:T(8,128)(2,1)} %dynamic-slice_bitcast_fusion), channel_id=1, source_target_pairs={{0,8},{8,0},{1,9},{9,1},{2,10},{10,2},{3,11},{11,3},{4,12},{12,4},... | collective-permute-start | bytes 4718600 | tf_op jit(solution)/shard_map/ppermute | solution.py:18
  81.8 25.6 %collective-permute-start.9 = (bf16[256,2048]{1,0:T(8,128)(2,1)}, bf16[256,2048]{1,0:T(8,128)(2,1)}, u32[]{:S(2)}, u32[]{:S(2)}) collective-permute-start(bf16[256,2048]{1,0:T(8,128)(2,1)} %get-tuple-element.15), channel_id=1, source_target_pairs={{0,2},{2,0},{4,6},{6,4},{1,3},{3,1},{5,7},{7,5},{8,10},{10,8},{12,... | collective-permute-start | bytes 3145736 | tf_op jit(solution)/shard_map/ppermute | solution.py:18
  84.3 19.7 %collective-permute-start.22 = (bf16[4,128,768]{2,1,0:T(8,128)(2,1)}, bf16[4,128,768]{2,1,0:T(8,128)(2,1)}, u32[]{:S(2)}, u32[]{:S(2)}) collective-permute-start(bf16[4,128,768]{2,1,0:T(8,128)(2,1)} %fusion.1), channel_id=1, source_target_pairs={{0,16},{16,0},{32,48},{48,32},{64,80},{80,64},{96,112},{112,96},{1... | collective-permute-start | bytes 2359304 | tf_op jit(solution)/shard_map/ppermute | solution.py:18
  86.2 44.7 %collective-permute-start.7 = (bf16[256,2048]{1,0:T(8,128)(2,1)}, bf16[256,2048]{1,0:T(8,128)(2,1)}, u32[]{:S(2)}, u32[]{:S(2)}) collective-permute-start(bf16[256,2048]{1,0:T(8,128)(2,1)} %get-tuple-element.13), channel_id=1, source_target_pairs={{0,6},{2,4},{4,2},{6,0},{1,7},{3,5},{5,3},{7,1},{8,14},{10,12},{12... | collective-permute-start | bytes 3145736 | tf_op jit(solution)/shard_map/ppermute | solution.py:18
  98.3 35.2 %collective-permute-start.27 = (bf16[4,128,768]{2,1,0:T(8,128)(2,1)S(1)}, bf16[4,128,768]{2,1,0:T(8,128)(2,1)S(1)}, u32[]{:S(2)}, u32[]{:S(2)}) collective-permute-start(bf16[4,128,768]{2,1,0:T(8,128)(2,1)S(1)} %fusion), channel_id=1, source_target_pairs={{0,112},{16,32},{32,16},{48,64},{64,48},{80,96},{96,80},{112,0},{1... | collective-permute-start | bytes 2359304 | tf_op jit(solution)/shard_map/ppermute | solution.py:18
  105.2 19.0 %collective-permute-start.23 = (bf16[128,768]{1,0:T(8,128)(2,1)S(1)}, bf16[128,768]{1,0:T(8,128)(2,1)S(1)}, u32[]{:S(2)}, u32[]{:S(2)}) collective-permute-start(bf16[128,768]{1,0:T(8,128)(2,1)S(1)} %fusion.15), channel_id=1, source_target_pairs={{0,32},{16,48},{32,0},{48,16},{64,96},{80,112},{96,64},{112,80},{1... | collective-permute-start | bytes 589832 | tf_op jit(solution)/shard_map/ppermute | solution.py:18
  108.6 40.4 %collective-permute-start.10 = (bf16[128,2048]{1,0:T(8,128)(2,1)S(1)}, bf16[128,2048]{1,0:T(8,128)(2,1)S(1)}, u32[]{:S(2)}, u32[]{:S(2)}) collective-permute-start(bf16[128,2048]{1,0:T(8,128)(2,1)S(1)} %add_convert_fusion.1), channel_id=1, source_target_pairs={{0,6},{2,4},{4,2},{6,0},{1,7},{3,5},{5,3},{7,1},{8,14},{10,12},{12... | collective-permute-start | bytes 1572872 | tf_op jit(solution)/shard_map/ppermute | solution.py:18
  125.2 18.4 %collective-permute-start.24 = (bf16[128,768]{1,0:T(8,128)(2,1)S(1)}, bf16[128,768]{1,0:T(8,128)(2,1)S(1)}, u32[]{:S(2)}, u32[]{:S(2)}) collective-permute-start(bf16[128,768]{1,0:T(8,128)(2,1)S(1)} %fusion.14), channel_id=1, source_target_pairs={{0,96},{16,112},{32,64},{48,80},{64,32},{80,48},{96,0},{112,16},{1... | collective-permute-start | bytes 589832 | tf_op jit(solution)/shard_map/ppermute | solution.py:18
  132.1 34.2 %collective-permute-start.8 = (bf16[128,2048]{1,0:T(8,128)(2,1)S(1)}, bf16[128,2048]{1,0:T(8,128)(2,1)S(1)}, u32[]{:S(2)}, u32[]{:S(2)}) collective-permute-start(bf16[128,2048]{1,0:T(8,128)(2,1)S(1)} %add_convert_fusion.4), channel_id=1, source_target_pairs={{0,2},{2,0},{4,6},{6,4},{1,3},{3,1},{5,7},{7,5},{8,10},{10,8},{12,... | collective-permute-start | bytes 1572872 | tf_op jit(solution)/shard_map/ppermute | solution.py:18
  134.6 12.8 %collective-permute-start.28 = (bf16[128,768]{1,0:T(8,128)(2,1)S(1)}, bf16[128,768]{1,0:T(8,128)(2,1)S(1)}, u32[]{:S(2)}, u32[]{:S(2)}) collective-permute-start(bf16[128,768]{1,0:T(8,128)(2,1)S(1)} %fusion.8), channel_id=1, source_target_pairs={{0,96},{16,112},{32,64},{48,80},{64,32},{80,48},{96,0},{112,16},{1... | collective-permute-start | bytes 589832 | tf_op jit(solution)/shard_map/ppermute | solution.py:18
  144.8 22.8 %collective-permute-start.25 = (bf16[128,768]{1,0:T(8,128)(2,1)S(1)}, bf16[128,768]{1,0:T(8,128)(2,1)S(1)}, u32[]{:S(2)}, u32[]{:S(2)}) collective-permute-start(bf16[128,768]{1,0:T(8,128)(2,1)S(1)} %fusion.12), channel_id=1, source_target_pairs={{0,32},{16,48},{32,0},{48,16},{64,96},{80,112},{96,64},{112,80},{1... | collective-permute-start | bytes 589832 | tf_op jit(solution)/shard_map/ppermute | solution.py:18
  148.5 12.7 %collective-permute-start.29 = (bf16[128,768]{1,0:T(8,128)(2,1)S(1)}, bf16[128,768]{1,0:T(8,128)(2,1)S(1)}, u32[]{:S(2)}, u32[]{:S(2)}) collective-permute-start(bf16[128,768]{1,0:T(8,128)(2,1)S(1)} %fusion.7), channel_id=1, source_target_pairs={{0,32},{16,48},{32,0},{48,16},{64,96},{80,112},{96,64},{112,80},{1... | collective-permute-start | bytes 589832 | tf_op jit(solution)/shard_map/ppermute | solution.py:18
  150.3 29.7 %collective-permute-start.11 = (bf16[128,2048]{1,0:T(8,128)(2,1)S(1)}, bf16[128,2048]{1,0:T(8,128)(2,1)S(1)}, u32[]{:S(2)}, u32[]{:S(2)}) collective-permute-start(bf16[128,2048]{1,0:T(8,128)(2,1)S(1)} %add_convert_fusion), channel_id=1, source_target_pairs={{0,1},{1,0},{2,3},{3,2},{4,5},{5,4},{6,7},{7,6},{8,9},{9,8},{10,11... | collective-permute-start | bytes 1572872 | tf_op jit(solution)/shard_map/ppermute | solution.py:18
  162.3 11.8 %collective-permute-start.30 = (bf16[128,768]{1,0:T(8,128)(2,1)S(1)}, bf16[128,768]{1,0:T(8,128)(2,1)S(1)}, u32[]{:S(2)}, u32[]{:S(2)}) collective-permute-start(bf16[128,768]{1,0:T(8,128)(2,1)S(1)} %fusion.5), channel_id=1, source_target_pairs={{0,96},{16,112},{32,64},{48,80},{64,32},{80,48},{96,0},{112,16},{1... | collective-permute-start | bytes 589832 | tf_op jit(solution)/shard_map/ppermute | solution.py:18
  178.0 7.6 %collective-permute-start.31 = (bf16[128,768]{1,0:T(8,128)(2,1)S(1)}, bf16[128,768]{1,0:T(8,128)(2,1)S(1)}, u32[]{:S(2)}, u32[]{:S(2)}) collective-permute-start(bf16[128,768]{1,0:T(8,128)(2,1)S(1)} %get-tuple-element.16), channel_id=1, source_target_pairs={{0,0},{1,128},{128,1},{129,129},{2,2},{3,130},{130,3},{131,131},{4... | collective-permute-start | bytes 589832 | tf_op jit(solution)/shard_map/ppermute | solution.py:281
  (12 other events, 155.8 us)

commit v2 on v1

--- a/solution.py
+++ b/solution.py
@@ -280,12 +280,16 @@
     away = [(2 * a + b, 2 * b + 1 - a) for a in range(2) for b in range(2)]
     first = lax.ppermute(first, ("yh", "yl"), home)
     second = lax.ppermute(second, ("yh", "yl"), away)
-    weight_grad = first.astype(F32) + second.astype(F32)
+
+    def added(start, width):
+        left, right = first[:, start : start + width], second[:, start : start + width]
+        return left.astype(F32) + right.astype(F32)
+
     return (
         hidden_grad,
-        weight_grad[:, :q_cols],
-        weight_grad[:, q_cols : q_cols + k_cols],
-        weight_grad[:, q_cols + k_cols :],
+        added(0, q_cols),
+        added(q_cols, k_cols),
+        added(q_cols + k_cols, k_cols),
     )
 
 

time: 188 us -> 188 us (level)
  no operation moved by 1% of the time
where the time goes in v2:
time: 188 us; the launch traced here: 187 us
  waiting for transfers between devices  76.8 us (41%)
  starting transfers between devices  48.6 us (26%)
  Pallas kernels  22.4 us (12%)
  other arithmetic  20.5 us (11%)
  matrix products  9.06 us (5%)
  local copies, waits for them, and re-layouts  8.59 us (5%)
    ppermute x31, waiting for transfers between devices, swap(): return lax.ppermute(value, axis, [(i, partner(i)) for i in range(size)])  72.4 us
    ppermute x31, starting transfers between devices, swap(): return lax.ppermute(value, axis, [(i, partner(i)) for i in range(size)])  44.3 us
    pallas_call x2, Pallas kernels, input_product(): pl.pallas_call(body, out_shape=[jax.ShapeDtypeStruct((n_rows // 2, steps...  16.6 us
    dot_general x2, matrix products, dot_rows(): lax.dot_general(left, right, (((0,), (0,)), ((), ())), preferred_element_...  9.06 us
    convert_element_type x4, other arithmetic, plus(): return (left.astype(F32) + right.astype(F32)).astype(BF16)  4.89 us
    convert_element_type x4, other arithmetic, ring(): passed = (taken.astype(F32) + chunk(step)).astype(BF16)  4.49 us
    ppermute x1, waiting for transfers between devices, body(): first = lax.ppermute(first, ('yh', 'yl'), home)  4.18 us
    pallas_call x1, Pallas kernels, ordered(): pl.pallas_call(body, name='ordered', out_shape=[out, out], grid_spec=pltp...  4.02 us
  transfers between devices with their start and end apart: 33, of which 16 were waited for; matrix products, arithmetic and copies ran while one was open for 18% of the time, Pallas kernels for 12%

profile of v2, /device:TPU:46, one launch (start us, length us, event | category | flops | bytes accessed | tf_op | source)
XLA Modules:
  0.0 187.0 jit_solution(15516651728575146676)
XLA Ops:
  0.6 2.1 %constant_dynamic-slice_fusion = (bf16[128,2048]{1,0:T(8,128)(2,1)}, bf16[128,2048]{1,0:T(8,128)(2,1)S(1)}) fusion(bf16[128,4096]{1,0:T(8,128)(2,1)} %param.7, s32[]{:T(128)S(6)} %select_n.225, s32[]{:T(128)S(6)} %select_n.224), kind=kLoop, calls=%fused_computation.65 | loop fusion | bytes 2097160 | tf_op jit(solution)/shard_map/dynamic_slice | solution.py:165
  8.8 4.0 %ordered.1 = (bf16[1024,768]{1,0:T(8,128)(2,1)}, bf16[1024,768]{1,0:T(8,128)(2,1)}) custom-call(s32[16]{0:T(128)} %concatenate.19.table, bf16[1024,512]{1,0:T(8,128)(2,1)} %refs_0_.2, bf16[1024,128]{1,0:T(8,128)(2,1)} %refs_1_.2, bf16[1024,128]{1,0:T(8,128)(2,1)} %refs_2_.2), custom_call_target="tpu_custom_call" | custom-call | tf_op jit(solution)/shard_map/ordered/pallas_call | solution.py:70
  13.3 4.3 %collective-permute-done.12 = bf16[128,2048]{1,0:T(8,128)(2,1)S(1)} collective-permute-done((bf16[128,2048]{1,0:T(8,128)(2,1)S(1)}, bf16[128,2048]{1,0:T(8,128)(2,1)S(1)}, u32[]{:S(2)}, u32[]{:S(2)}) %collective-permute-start.12) | collective-permute-done | bytes 524320 | tf_op jit(solution)/shard_map/ppermute | solution.py:18
  18.3 2.2 %collective-permute-start.15 = (bf16[64,2048]{1,0:T(8,128)(2,1)S(1)}, bf16[64,2048]{1,0:T(8,128)(2,1)S(1)}, u32[]{:S(2)}, u32[]{:S(2)}) collective-permute-start(bf16[64,2048]{1,0:T(8,128)(2,1)S(1)} %slice.87), channel_id=1, source_target_pairs={{0,6},{2,4},{4,2},{6,0},{1,7},{3,5},{5,3},{7,1},{8,14},{10,12},{12... | collective-permute-start | bytes 786440 | tf_op jit(solution)/shard_map/ppermute | solution.py:18
  20.6 8.9 %collective-permute-done.16 = bf16[128,2048]{1,0:T(8,128)(2,1)} collective-permute-done((bf16[128,2048]{1,0:T(8,128)(2,1)}, bf16[128,2048]{1,0:T(8,128)(2,1)}, u32[]{:S(2)}, u32[]{:S(2)}) %collective-permute-start.16) | collective-permute-done | bytes 524320 | tf_op jit(solution)/shard_map/ppermute | solution.py:18
  29.4 1.9 %collective-permute-start.3 = (bf16[256,768]{1,0:T(8,128)(2,1)S(1)}, bf16[256,768]{1,0:T(8,128)(2,1)S(1)}, u32[]{:S(2)}, u32[]{:S(2)}) collective-permute-start(bf16[256,768]{1,0:T(8,128)(2,1)S(1)} %collective-permute-done.1), channel_id=1, source_target_pairs={{0,112},{16,32},{32,16},{48,64},{64,48},{80,96},{96,80},{112,0},{1... | collective-permute-start | bytes 1179656 | tf_op jit(solution)/shard_map/ppermute | solution.py:18
  32.5 2.8 %collective-permute-start.18 = (bf16[128,2048]{1,0:T(8,128)(2,1)}, bf16[128,2048]{1,0:T(8,128)(2,1)S(1)}, u32[]{:S(2)}, u32[]{:S(2)}) collective-permute-start(bf16[128,2048]{1,0:T(8,128)(2,1)} %collective-permute-done.16), channel_id=1, source_target_pairs={{0,6},{2,4},{4,2},{6,0},{1,7},{3,5},{5,3},{7,1},{8,14},{10,12},{12... | collective-permute-start | bytes 1572872 | tf_op jit(solution)/shard_map/ppermute | solution.py:18
  35.4 1.9 %collective-permute-done.3 = bf16[256,768]{1,0:T(8,128)(2,1)S(1)} collective-permute-done((bf16[256,768]{1,0:T(8,128)(2,1)S(1)}, bf16[256,768]{1,0:T(8,128)(2,1)S(1)}, u32[]{:S(2)}, u32[]{:S(2)}) %collective-permute-start.3) | collective-permute-done | bytes 393248 | tf_op jit(solution)/shard_map/ppermute | solution.py:18
  37.4 4.1 %collective-permute-start.4 = (bf16[128,768]{1,0:T(8,128)(2,1)S(1)}, bf16[128,768]{1,0:T(8,128)(2,1)S(1)}, u32[]{:S(2)}, u32[]{:S(2)}) collective-permute-start(bf16[128,768]{1,0:T(8,128)(2,1)S(1)} %slice.80), channel_id=1, source_target_pairs={{0,16},{16,0},{32,48},{48,32},{64,80},{80,64},{96,112},{112,96},{1... | collective-permute-start | bytes 589832 | tf_op jit(solution)/shard_map/ppermute | solution.py:18
  42.7 2.5 %collective-permute-done.4 = bf16[128,768]{1,0:T(8,128)(2,1)S(1)} collective-permute-done((bf16[128,768]{1,0:T(8,128)(2,1)S(1)}, bf16[128,768]{1,0:T(8,128)(2,1)S(1)}, u32[]{:S(2)}, u32[]{:S(2)}) %collective-permute-start.4) | collective-permute-done | bytes 196640 | tf_op jit(solution)/shard_map/ppermute | solution.py:18
  47.5 2.5 %collective-permute-start.20 = (bf16[64,2048]{1,0:T(8,128)(2,1)S(1)}, bf16[64,2048]{1,0:T(8,128)(2,1)S(1)}, u32[]{:S(2)}, u32[]{:S(2)}) collective-permute-start(bf16[64,2048]{1,0:T(8,128)(2,1)S(1)} %slice.89), channel_id=1, source_target_pairs={{0,6},{2,4},{4,2},{6,0},{1,7},{3,5},{5,3},{7,1},{8,14},{10,12},{12... | collective-permute-start | bytes 786440 | tf_op jit(solution)/shard_map/ppermute | solution.py:18
  51.7 6.0 %collective-permute-done.20 = bf16[64,2048]{1,0:T(8,128)(2,1)S(1)} collective-permute-done((bf16[64,2048]{1,0:T(8,128)(2,1)S(1)}, bf16[64,2048]{1,0:T(8,128)(2,1)S(1)}, u32[]{:S(2)}, u32[]{:S(2)}) %collective-permute-start.20) | collective-permute-done | bytes 262176 | tf_op jit(solution)/shard_map/ppermute | solution.py:18
  58.9 3.7 %convolution_convert_fusion.1 = bf16[2048,768]{1,0:T(8,128)(2,1)S(1)} fusion(bf16[1024,2048]{1,0:T(8,128)(2,1)S(1)} %constant_dynamic-update-slice_fusion.5, bf16[1024,768]{1,0:T(8,128)(2,1)S(1)} %copy-done.1), kind=kOutput, calls=%fused_computation.1 | convolution fusion | flops 3222798336 | bytes 8912896 | tf_op jit(solution)/shard_map/dot_general | solution.py:130
  64.1 5.3 %convolution_convert_fusion = bf16[2048,768]{1,0:T(8,128)(2,1)S(1)} fusion(bf16[1024,2048]{1,0:T(8,128)(2,1)S(1)} %constant_dynamic-update-slice_fusion.5, bf16[1024,768]{1,0:T(8,128)(2,1)} %collective-permute-done.got), kind=kOutput, calls=%fused_computation | convolution fusion | flops 3222798336 | bytes 8912896 | tf_op jit(solution)/shard_map/dot_general | solution.py:130
  73.3 8.5 %shard_map.103 = (bf16[256,2048]{1,0:T(8,128)(2,1)}, bf16[256,2048]{1,0:T(8,128)(2,1)}) custom-call(s32[9]{0:T(128)} %pad_add_fusion.table, bf16[1024,768]{1,0:T(8,128)(2,1)} %get-tuple-element.10.mine, bf16[1024,768]{1,0:T(8,128)(2,1)} %collective-permute-done.got, bf16[4096,512]{1,0:T(8,128)(2,1)} %q.3, bf16[4096,128]{1,0:T(8,128)(2,1)} %k.3, ...), custom_call_target="tpu_custom_call" | custom-call | flops 3221225472 | bytes 6291456 | tf_op jit(solution)/shard_map/pallas_call | solution.py:109
  82.1 2.2 %fusion.1 = bf16[4,128,768]{2,1,0:T(8,128)(2,1)} fusion(bf16[4,2,128,768]{3,2,1,0:T(8,128)(2,1)} %bitcast.10, s32[]{:T(128)S(6)} %select_n.234, bf16[4,2,2,128,768]{4,3,2,1,0:T(8,128)(2,1)S(1)} %bitcast.115, s32[]{:T(128)S(6)} %select_n.232), kind=kLoop, calls=%fused_computation.5 | loop fusion | flops 1572864 | bytes 2359304 | tf_op jit(solution)/shard_map/convert_element_type | solution.py:236
  84.3 1.8 collective-permute-start.22
  86.2 2.3 %collective-permute-start.7 = (bf16[256,2048]{1,0:T(8,128)(2,1)}, bf16[256,2048]{1,0:T(8,128)(2,1)}, u32[]{:S(2)}, u32[]{:S(2)}) collective-permute-start(bf16[256,2048]{1,0:T(8,128)(2,1)} %get-tuple-element.13), channel_id=1, source_target_pairs={{0,6},{2,4},{4,2},{6,0},{1,7},{3,5},{5,3},{7,1},{8,14},{10,12},{12... | collective-permute-start | bytes 3145736 | tf_op jit(solution)/shard_map/ppermute | solution.py:18
  88.5 8.1 %shard_map.102 = (bf16[256,2048]{1,0:T(8,128)(2,1)}, bf16[256,2048]{1,0:T(8,128)(2,1)}) custom-call(s32[9]{0:T(128)} %pad_add_fusion.table, bf16[1024,768]{1,0:T(8,128)(2,1)} %get-tuple-element.10.mine, bf16[1024,768]{1,0:T(8,128)(2,1)} %collective-permute-done.got, bf16[4096,512]{1,0:T(8,128)(2,1)} %q.3, bf16[4096,128]{1,0:T(8,128)(2,1)} %k.3, ...), custom_call_target="tpu_custom_call" | custom-call | flops 3221225472 | bytes 6291456 | tf_op jit(solution)/shard_map/pallas_call | solution.py:109
  99.4 4.6 %collective-permute-done.22 = bf16[4,128,768]{2,1,0:T(8,128)(2,1)} collective-permute-done((bf16[4,128,768]{2,1,0:T(8,128)(2,1)}, bf16[4,128,768]{2,1,0:T(8,128)(2,1)}, u32[]{:S(2)}, u32[]{:S(2)}) %collective-permute-start.22) | collective-permute-done | bytes 786464 | tf_op jit(solution)/shard_map/ppermute | solution.py:18
  105.2 2.3 %collective-permute-start.23 = (bf16[128,768]{1,0:T(8,128)(2,1)S(1)}, bf16[128,768]{1,0:T(8,128)(2,1)S(1)}, u32[]{:S(2)}, u32[]{:S(2)}) collective-permute-start(bf16[128,768]{1,0:T(8,128)(2,1)S(1)} %fusion.15), channel_id=1, source_target_pairs={{0,32},{16,48},{32,0},{48,16},{64,96},{80,112},{96,64},{112,80},{1... | collective-permute-start | bytes 589832 | tf_op jit(solution)/shard_map/ppermute | solution.py:18
  108.6 2.4 %collective-permute-start.10 = (bf16[128,2048]{1,0:T(8,128)(2,1)S(1)}, bf16[128,2048]{1,0:T(8,128)(2,1)S(1)}, u32[]{:S(2)}, u32[]{:S(2)}) collective-permute-start(bf16[128,2048]{1,0:T(8,128)(2,1)S(1)} %add_convert_fusion.1), channel_id=1, source_target_pairs={{0,6},{2,4},{4,2},{6,0},{1,7},{3,5},{5,3},{7,1},{8,14},{10,12},{12... | collective-permute-start | bytes 1572872 | tf_op jit(solution)/shard_map/ppermute | solution.py:18
  111.0 13.1 %collective-permute-done.23 = bf16[128,768]{1,0:T(8,128)(2,1)S(1)} collective-permute-done((bf16[128,768]{1,0:T(8,128)(2,1)S(1)}, bf16[128,768]{1,0:T(8,128)(2,1)S(1)}, u32[]{:S(2)}, u32[]{:S(2)}) %collective-permute-start.23) | collective-permute-done | bytes 196640 | tf_op jit(solution)/shard_map/ppermute | solution.py:18
  125.2 5.7 %collective-permute-start.24 = (bf16[128,768]{1,0:T(8,128)(2,1)S(1)}, bf16[128,768]{1,0:T(8,128)(2,1)S(1)}, u32[]{:S(2)}, u32[]{:S(2)}) collective-permute-start(bf16[128,768]{1,0:T(8,128)(2,1)S(1)} %fusion.14), channel_id=1, source_target_pairs={{0,96},{16,112},{32,64},{48,80},{64,32},{80,48},{96,0},{112,16},{1... | collective-permute-start | bytes 589832 | tf_op jit(solution)/shard_map/ppermute | solution.py:18
  134.7 8.9 %collective-permute-done.24 = bf16[128,768]{1,0:T(8,128)(2,1)S(1)} collective-permute-done((bf16[128,768]{1,0:T(8,128)(2,1)S(1)}, bf16[128,768]{1,0:T(8,128)(2,1)S(1)}, u32[]{:S(2)}, u32[]{:S(2)}) %collective-permute-start.24) | collective-permute-done | bytes 196640 | tf_op jit(solution)/shard_map/ppermute | solution.py:18
  145.1 2.2 %collective-permute-done.28 = bf16[128,768]{1,0:T(8,128)(2,1)S(1)} collective-permute-done((bf16[128,768]{1,0:T(8,128)(2,1)S(1)}, bf16[128,768]{1,0:T(8,128)(2,1)S(1)}, u32[]{:S(2)}, u32[]{:S(2)}) %collective-permute-start.28) | collective-permute-done | bytes 196640 | tf_op jit(solution)/shard_map/ppermute | solution.py:18
  150.8 10.4 %collective-permute-done.29 = bf16[128,768]{1,0:T(8,128)(2,1)S(1)} collective-permute-done((bf16[128,768]{1,0:T(8,128)(2,1)S(1)}, bf16[128,768]{1,0:T(8,128)(2,1)S(1)}, u32[]{:S(2)}, u32[]{:S(2)}) %collective-permute-start.29) | collective-permute-done | bytes 196640 | tf_op jit(solution)/shard_map/ppermute | solution.py:18
  162.3 3.9 %collective-permute-start.30 = (bf16[128,768]{1,0:T(8,128)(2,1)S(1)}, bf16[128,768]{1,0:T(8,128)(2,1)S(1)}, u32[]{:S(2)}, u32[]{:S(2)}) collective-permute-start(bf16[128,768]{1,0:T(8,128)(2,1)S(1)} %fusion.5), channel_id=1, source_target_pairs={{0,96},{16,112},{32,64},{48,80},{64,32},{80,48},{96,0},{112,16},{1... | collective-permute-start | bytes 589832 | tf_op jit(solution)/shard_map/ppermute | solution.py:18
  167.6 6.6 %collective-permute-done.30 = bf16[128,768]{1,0:T(8,128)(2,1)S(1)} collective-permute-done((bf16[128,768]{1,0:T(8,128)(2,1)S(1)}, bf16[128,768]{1,0:T(8,128)(2,1)S(1)}, u32[]{:S(2)}, u32[]{:S(2)}) %collective-permute-start.30) | collective-permute-done | bytes 196640 | tf_op jit(solution)/shard_map/ppermute | solution.py:18
  175.7 2.4 %collective-permute-start.32 = (bf16[128,768]{1,0:T(8,128)(2,1)S(1)}, bf16[128,768]{1,0:T(8,128)(2,1)S(1)}, u32[]{:S(2)}, u32[]{:S(2)}) collective-permute-start(bf16[128,768]{1,0:T(8,128)(2,1)S(1)} %broadcast_select_fusion), channel_id=1, source_target_pairs={{0,1},{1,129},{128,0},{129,128},{2,3},{3,131},{130,2},{131,130},{4... | collective-permute-start | bytes 589832 | tf_op jit(solution)/shard_map/ppermute | solution.py:282
  178.0 1.9 %collective-permute-start.31 = (bf16[128,768]{1,0:T(8,128)(2,1)S(1)}, bf16[128,768]{1,0:T(8,128)(2,1)S(1)}, u32[]{:S(2)}, u32[]{:S(2)}) collective-permute-start(bf16[128,768]{1,0:T(8,128)(2,1)S(1)} %get-tuple-element.16), channel_id=1, source_target_pairs={{0,0},{1,128},{128,1},{129,129},{2,2},{3,130},{130,3},{131,131},{4... | collective-permute-start | bytes 589832 | tf_op jit(solution)/shard_map/ppermute | solution.py:281
  181.4 4.2 %collective-permute-done.31 = bf16[128,768]{1,0:T(8,128)(2,1)S(1)} collective-permute-done((bf16[128,768]{1,0:T(8,128)(2,1)S(1)}, bf16[128,768]{1,0:T(8,128)(2,1)S(1)}, u32[]{:S(2)}, u32[]{:S(2)}) %collective-permute-start.31) | collective-permute-done | bytes 196640 | tf_op jit(solution)/shard_map/ppermute | solution.py:281
  (111 shorter events, 42.0 us)
Async XLA Ops:
  2.7 14.9 %collective-permute-start.12 = (bf16[128,2048]{1,0:T(8,128)(2,1)S(1)}, bf16[128,2048]{1,0:T(8,128)(2,1)S(1)}, u32[]{:S(2)}, u32[]{:S(2)}) collective-permute-start(bf16[128,2048]{1,0:T(8,128)(2,1)S(1)} %get-tuple-element.20), channel_id=1, source_target_pairs={{0,6},{2,4},{4,2},{6,0},{1,7},{3,5},{5,3},{7,1},{8,14},{10,12},{12... | collective-permute-start | bytes 1572872 | tf_op jit(solution)/shard_map/ppermute | solution.py:18
  3.2 15.1 %collective-permute-start.14 = (bf16[128,2048]{1,0:T(8,128)(2,1)S(1)}, bf16[128,2048]{1,0:T(8,128)(2,1)S(1)}, u32[]{:S(2)}, u32[]{:S(2)}) collective-permute-start(bf16[128,2048]{1,0:T(8,128)(2,1)S(1)} %get-tuple-element.20), channel_id=1, source_target_pairs={{0,2},{2,0},{4,6},{6,4},{1,3},{3,1},{5,7},{7,5},{8,10},{10,8},{12,... | collective-permute-start | bytes 1572872 | tf_op jit(solution)/shard_map/ppermute | solution.py:18
  5.9 12.2 %collective-permute-start.1 = (bf16[256,768]{1,0:T(8,128)(2,1)}, bf16[256,768]{1,0:T(8,128)(2,1)S(1)}, u32[]{:S(2)}, u32[]{:S(2)}) collective-permute-start(bf16[256,768]{1,0:T(8,128)(2,1)} %cut.1), channel_id=1, source_target_pairs={{0,1},{1,0},{2,3},{3,2},{4,5},{5,4},{6,7},{7,6},{8,9},{9,8},{10,11... | collective-permute-start | bytes 1179656 | tf_op jit(solution)/shard_map/ppermute | solution.py:18
  6.3 23.1 %collective-permute-start.16 = (bf16[128,2048]{1,0:T(8,128)(2,1)}, bf16[128,2048]{1,0:T(8,128)(2,1)}, u32[]{:S(2)}, u32[]{:S(2)}) collective-permute-start(bf16[128,2048]{1,0:T(8,128)(2,1)} %get-tuple-element.19), channel_id=1, source_target_pairs={{0,1},{1,0},{2,3},{3,2},{4,5},{5,4},{6,7},{7,6},{8,9},{9,8},{10,11... | collective-permute-start | bytes 1572872 | tf_op jit(solution)/shard_map/ppermute | solution.py:18
  12.9 51.2 %collective-permute-start = (bf16[1024,768]{1,0:T(8,128)(2,1)}, bf16[1024,768]{1,0:T(8,128)(2,1)}, u32[]{:S(2)}, u32[]{:S(2)}) collective-permute-start(bf16[1024,768]{1,0:T(8,128)(2,1)} %get-tuple-element.11), channel_id=1, source_target_pairs={{0,1},{1,0},{2,3},{3,2},{4,5},{5,4},{6,7},{7,6},{8,9},{9,8},{10,11... | collective-permute-start | bytes 4718600 | tf_op jit(solution)/shard_map/ppermute | solution.py:18
  17.6 13.7 %collective-permute-start.13 = (bf16[64,2048]{1,0:T(8,128)(2,1)S(1)}, bf16[64,2048]{1,0:T(8,128)(2,1)S(1)}, u32[]{:S(2)}, u32[]{:S(2)}) collective-permute-start(bf16[64,2048]{1,0:T(8,128)(2,1)S(1)} %slice.86), channel_id=1, source_target_pairs={{0,2},{2,0},{4,6},{6,4},{1,3},{3,1},{5,7},{7,5},{8,10},{10,8},{12,... | collective-permute-start | bytes 786440 | tf_op jit(solution)/shard_map/ppermute | solution.py:18
  18.1 23.4 %collective-permute-start.2 = (bf16[256,768]{1,0:T(8,128)(2,1)S(1)}, bf16[256,768]{1,0:T(8,128)(2,1)S(1)}, u32[]{:S(2)}, u32[]{:S(2)}) collective-permute-start(bf16[256,768]{1,0:T(8,128)(2,1)S(1)} %collective-permute-done.1), channel_id=1, source_target_pairs={{0,16},{16,0},{32,48},{48,32},{64,80},{80,64},{96,112},{112,96},{1... | collective-permute-start | bytes 1179656 | tf_op jit(solution)/shard_map/ppermute | solution.py:18
  18.3 14.2 %collective-permute-start.15 = (bf16[64,2048]{1,0:T(8,128)(2,1)S(1)}, bf16[64,2048]{1,0:T(8,128)(2,1)S(1)}, u32[]{:S(2)}, u32[]{:S(2)}) collective-permute-start(bf16[64,2048]{1,0:T(8,128)(2,1)S(1)} %slice.87), channel_id=1, source_target_pairs={{0,6},{2,4},{4,2},{6,0},{1,7},{3,5},{5,3},{7,1},{8,14},{10,12},{12... | collective-permute-start | bytes 786440 | tf_op jit(solution)/shard_map/ppermute | solution.py:18
  29.4 7.9 %collective-permute-start.3 = (bf16[256,768]{1,0:T(8,128)(2,1)S(1)}, bf16[256,768]{1,0:T(8,128)(2,1)S(1)}, u32[]{:S(2)}, u32[]{:S(2)}) collective-permute-start(bf16[256,768]{1,0:T(8,128)(2,1)S(1)} %collective-permute-done.1), channel_id=1, source_target_pairs={{0,112},{16,32},{32,16},{48,64},{64,48},{80,96},{96,80},{112,0},{1... | collective-permute-start | bytes 1179656 | tf_op jit(solution)/shard_map/ppermute | solution.py:18
  31.4 16.1 %collective-permute-start.17 = (bf16[128,2048]{1,0:T(8,128)(2,1)}, bf16[128,2048]{1,0:T(8,128)(2,1)S(1)}, u32[]{:S(2)}, u32[]{:S(2)}) collective-permute-start(bf16[128,2048]{1,0:T(8,128)(2,1)} %collective-permute-done.16), channel_id=1, source_target_pairs={{0,2},{2,0},{4,6},{6,4},{1,3},{3,1},{5,7},{7,5},{8,10},{10,8},{12,... | collective-permute-start | bytes 1572872 | tf_op jit(solution)/shard_map/ppermute | solution.py:18
  32.5 12.6 %collective-permute-start.18 = (bf16[128,2048]{1,0:T(8,128)(2,1)}, bf16[128,2048]{1,0:T(8,128)(2,1)S(1)}, u32[]{:S(2)}, u32[]{:S(2)}) collective-permute-start(bf16[128,2048]{1,0:T(8,128)(2,1)} %collective-permute-done.16), channel_id=1, source_target_pairs={{0,6},{2,4},{4,2},{6,0},{1,7},{3,5},{5,3},{7,1},{8,14},{10,12},{12... | collective-permute-start | bytes 1572872 | tf_op jit(solution)/shard_map/ppermute | solution.py:18
  37.4 7.8 %collective-permute-start.4 = (bf16[128,768]{1,0:T(8,128)(2,1)S(1)}, bf16[128,768]{1,0:T(8,128)(2,1)S(1)}, u32[]{:S(2)}, u32[]{:S(2)}) collective-permute-start(bf16[128,768]{1,0:T(8,128)(2,1)S(1)} %slice.80), channel_id=1, source_target_pairs={{0,16},{16,0},{32,48},{48,32},{64,80},{80,64},{96,112},{112,96},{1... | collective-permute-start | bytes 589832 | tf_op jit(solution)/shard_map/ppermute | solution.py:18
  41.5 5.8 %collective-permute-start.5 = (bf16[128,768]{1,0:T(8,128)(2,1)S(1)}, bf16[128,768]{1,0:T(8,128)(2,1)S(1)}, u32[]{:S(2)}, u32[]{:S(2)}) collective-permute-start(bf16[128,768]{1,0:T(8,128)(2,1)S(1)} %slice.81), channel_id=1, source_target_pairs={{0,112},{16,32},{32,16},{48,64},{64,48},{80,96},{96,80},{112,0},{1... | collective-permute-start | bytes 589832 | tf_op jit(solution)/shard_map/ppermute | solution.py:18
  45.2 6.5 %collective-permute-start.19 = (bf16[64,2048]{1,0:T(8,128)(2,1)S(1)}, bf16[64,2048]{1,0:T(8,128)(2,1)S(1)}, u32[]{:S(2)}, u32[]{:S(2)}) collective-permute-start(bf16[64,2048]{1,0:T(8,128)(2,1)S(1)} %slice.88), channel_id=1, source_target_pairs={{0,2},{2,0},{4,6},{6,4},{1,3},{3,1},{5,7},{7,5},{8,10},{10,8},{12,... | collective-permute-start | bytes 786440 | tf_op jit(solution)/shard_map/ppermute | solution.py:18
  47.3 26.0 %collective-permute-start.6 = (bf16[1024,768]{1,0:T(8,128)(2,1)S(1)}, bf16[1024,768]{1,0:T(8,128)(2,1)}, u32[]{:S(2)}, u32[]{:S(2)}) collective-permute-start(bf16[1024,768]{1,0:T(8,128)(2,1)S(1)} %constant_dynamic-update-slice_fusion.pieces), channel_id=1, source_target_pairs={{0,8},{8,0},{1,9},{9,1},{2,10},{10,2},{3,11},{11,3},{4,12},{12,4},... | collective-permute-start | bytes 4718600 | tf_op jit(solution)/shard_map/ppermute | solution.py:18
  47.5 10.2 %collective-permute-start.20 = (bf16[64,2048]{1,0:T(8,128)(2,1)S(1)}, bf16[64,2048]{1,0:T(8,128)(2,1)S(1)}, u32[]{:S(2)}, u32[]{:S(2)}) collective-permute-start(bf16[64,2048]{1,0:T(8,128)(2,1)S(1)} %slice.89), channel_id=1, source_target_pairs={{0,6},{2,4},{4,2},{6,0},{1,7},{3,5},{5,3},{7,1},{8,14},{10,12},{12... | collective-permute-start | bytes 786440 | tf_op jit(solution)/shard_map/ppermute | solution.py:18
  64.1 18.0 %collective-permute-start.21 = (bf16[8,128,768]{2,1,0:T(8,128)(2,1)}, bf16[8,128,768]{2,1,0:T(8,128)(2,1)}, u32[]{:S(2)}, u32[]{:S(2)}) collective-permute-start(bf16[8,128,768]{2,1,0:T(8,128)(2,1)} %dynamic-slice_bitcast_fusion.1), channel_id=1, source_target_pairs={{0,8},{8,0},{1,9},{9,1},{2,10},{10,2},{3,11},{11,3},{4,12},{12,4},... | collective-permute-start | bytes 4718600 | tf_op jit(solution)/shard_map/ppermute | solution.py:18
  72.3 24.3 %collective-permute-start.26 = (bf16[8,128,768]{2,1,0:T(8,128)(2,1)}, bf16[8,128,768]{2,1,0:T(8,128)(2,1)}, u32[]{:S(2)}, u32[]{:S(2)}) collective-permute-start(bf16[8,128,768]{2,1,0:T(8,128)(2,1)} %dynamic-slice_bitcast_fusion), channel_id=1, source_target_pairs={{0,8},{8,0},{1,9},{9,1},{2,10},{10,2},{3,11},{11,3},{4,12},{12,4},... | collective-permute-start | bytes 4718600 | tf_op jit(solution)/shard_map/ppermute | solution.py:18
  81.8 25.6 %collective-permute-start.9 = (bf16[256,2048]{1,0:T(8,128)(2,1)}, bf16[256,2048]{1,0:T(8,128)(2,1)}, u32[]{:S(2)}, u32[]{:S(2)}) collective-permute-start(bf16[256,2048]{1,0:T(8,128)(2,1)} %get-tuple-element.15), channel_id=1, source_target_pairs={{0,2},{2,0},{4,6},{6,4},{1,3},{3,1},{5,7},{7,5},{8,10},{10,8},{12,... | collective-permute-start | bytes 3145736 | tf_op jit(solution)/shard_map/ppermute | solution.py:18
  84.3 19.7 %collective-permute-start.22 = (bf16[4,128,768]{2,1,0:T(8,128)(2,1)}, bf16[4,128,768]{2,1,0:T(8,128)(2,1)}, u32[]{:S(2)}, u32[]{:S(2)}) collective-permute-start(bf16[4,128,768]{2,1,0:T(8,128)(2,1)} %fusion.1), channel_id=1, source_target_pairs={{0,16},{16,0},{32,48},{48,32},{64,80},{80,64},{96,112},{112,96},{1... | collective-permute-start | bytes 2359304 | tf_op jit(solution)/shard_map/ppermute | solution.py:18
  86.2 44.7 %collective-permute-start.7 = (bf16[256,2048]{1,0:T(8,128)(2,1)}, bf16[256,2048]{1,0:T(8,128)(2,1)}, u32[]{:S(2)}, u32[]{:S(2)}) collective-permute-start(bf16[256,2048]{1,0:T(8,128)(2,1)} %get-tuple-element.13), channel_id=1, source_target_pairs={{0,6},{2,4},{4,2},{6,0},{1,7},{3,5},{5,3},{7,1},{8,14},{10,12},{12... | collective-permute-start | bytes 3145736 | tf_op jit(solution)/shard_map/ppermute | solution.py:18
  98.3 35.2 %collective-permute-start.27 = (bf16[4,128,768]{2,1,0:T(8,128)(2,1)S(1)}, bf16[4,128,768]{2,1,0:T(8,128)(2,1)S(1)}, u32[]{:S(2)}, u32[]{:S(2)}) collective-permute-start(bf16[4,128,768]{2,1,0:T(8,128)(2,1)S(1)} %fusion), channel_id=1, source_target_pairs={{0,112},{16,32},{32,16},{48,64},{64,48},{80,96},{96,80},{112,0},{1... | collective-permute-start | bytes 2359304 | tf_op jit(solution)/shard_map/ppermute | solution.py:18
  105.2 19.0 %collective-permute-start.23 = (bf16[128,768]{1,0:T(8,128)(2,1)S(1)}, bf16[128,768]{1,0:T(8,128)(2,1)S(1)}, u32[]{:S(2)}, u32[]{:S(2)}) collective-permute-start(bf16[128,768]{1,0:T(8,128)(2,1)S(1)} %fusion.15), channel_id=1, source_target_pairs={{0,32},{16,48},{32,0},{48,16},{64,96},{80,112},{96,64},{112,80},{1... | collective-permute-start | bytes 589832 | tf_op jit(solution)/shard_map/ppermute | solution.py:18
  108.6 40.4 %collective-permute-start.10 = (bf16[128,2048]{1,0:T(8,128)(2,1)S(1)}, bf16[128,2048]{1,0:T(8,128)(2,1)S(1)}, u32[]{:S(2)}, u32[]{:S(2)}) collective-permute-start(bf16[128,2048]{1,0:T(8,128)(2,1)S(1)} %add_convert_fusion.1), channel_id=1, source_target_pairs={{0,6},{2,4},{4,2},{6,0},{1,7},{3,5},{5,3},{7,1},{8,14},{10,12},{12... | collective-permute-start | bytes 1572872 | tf_op jit(solution)/shard_map/ppermute | solution.py:18
  125.2 18.4 %collective-permute-start.24 = (bf16[128,768]{1,0:T(8,128)(2,1)S(1)}, bf16[128,768]{1,0:T(8,128)(2,1)S(1)}, u32[]{:S(2)}, u32[]{:S(2)}) collective-permute-start(bf16[128,768]{1,0:T(8,128)(2,1)S(1)} %fusion.14), channel_id=1, source_target_pairs={{0,96},{16,112},{32,64},{48,80},{64,32},{80,48},{96,0},{112,16},{1... | collective-permute-start | bytes 589832 | tf_op jit(solution)/shard_map/ppermute | solution.py:18
  132.1 34.2 %collective-permute-start.8 = (bf16[128,2048]{1,0:T(8,128)(2,1)S(1)}, bf16[128,2048]{1,0:T(8,128)(2,1)S(1)}, u32[]{:S(2)}, u32[]{:S(2)}) collective-permute-start(bf16[128,2048]{1,0:T(8,128)(2,1)S(1)} %add_convert_fusion.4), channel_id=1, source_target_pairs={{0,2},{2,0},{4,6},{6,4},{1,3},{3,1},{5,7},{7,5},{8,10},{10,8},{12,... | collective-permute-start | bytes 1572872 | tf_op jit(solution)/shard_map/ppermute | solution.py:18
  134.6 12.8 %collective-permute-start.28 = (bf16[128,768]{1,0:T(8,128)(2,1)S(1)}, bf16[128,768]{1,0:T(8,128)(2,1)S(1)}, u32[]{:S(2)}, u32[]{:S(2)}) collective-permute-start(bf16[128,768]{1,0:T(8,128)(2,1)S(1)} %fusion.8), channel_id=1, source_target_pairs={{0,96},{16,112},{32,64},{48,80},{64,32},{80,48},{96,0},{112,16},{1... | collective-permute-start | bytes 589832 | tf_op jit(solution)/shard_map/ppermute | solution.py:18
  144.8 22.8 %collective-permute-start.25 = (bf16[128,768]{1,0:T(8,128)(2,1)S(1)}, bf16[128,768]{1,0:T(8,128)(2,1)S(1)}, u32[]{:S(2)}, u32[]{:S(2)}) collective-permute-start(bf16[128,768]{1,0:T(8,128)(2,1)S(1)} %fusion.12), channel_id=1, source_target_pairs={{0,32},{16,48},{32,0},{48,16},{64,96},{80,112},{96,64},{112,80},{1... | collective-permute-start | bytes 589832 | tf_op jit(solution)/shard_map/ppermute | solution.py:18
  148.5 12.7 %collective-permute-start.29 = (bf16[128,768]{1,0:T(8,128)(2,1)S(1)}, bf16[128,768]{1,0:T(8,128)(2,1)S(1)}, u32[]{:S(2)}, u32[]{:S(2)}) collective-permute-start(bf16[128,768]{1,0:T(8,128)(2,1)S(1)} %fusion.7), channel_id=1, source_target_pairs={{0,32},{16,48},{32,0},{48,16},{64,96},{80,112},{96,64},{112,80},{1... | collective-permute-start | bytes 589832 | tf_op jit(solution)/shard_map/ppermute | solution.py:18
  150.3 29.7 %collective-permute-start.11 = (bf16[128,2048]{1,0:T(8,128)(2,1)S(1)}, bf16[128,2048]{1,0:T(8,128)(2,1)S(1)}, u32[]{:S(2)}, u32[]{:S(2)}) collective-permute-start(bf16[128,2048]{1,0:T(8,128)(2,1)S(1)} %add_convert_fusion), channel_id=1, source_target_pairs={{0,1},{1,0},{2,3},{3,2},{4,5},{5,4},{6,7},{7,6},{8,9},{9,8},{10,11... | collective-permute-start | bytes 1572872 | tf_op jit(solution)/shard_map/ppermute | solution.py:18
  162.3 11.8 %collective-permute-start.30 = (bf16[128,768]{1,0:T(8,128)(2,1)S(1)}, bf16[128,768]{1,0:T(8,128)(2,1)S(1)}, u32[]{:S(2)}, u32[]{:S(2)}) collective-permute-start(bf16[128,768]{1,0:T(8,128)(2,1)S(1)} %fusion.5), channel_id=1, source_target_pairs={{0,96},{16,112},{32,64},{48,80},{64,32},{80,48},{96,0},{112,16},{1... | collective-permute-start | bytes 589832 | tf_op jit(solution)/shard_map/ppermute | solution.py:18
  178.0 7.6 %collective-permute-start.31 = (bf16[128,768]{1,0:T(8,128)(2,1)S(1)}, bf16[128,768]{1,0:T(8,128)(2,1)S(1)}, u32[]{:S(2)}, u32[]{:S(2)}) collective-permute-start(bf16[128,768]{1,0:T(8,128)(2,1)S(1)} %get-tuple-element.16), channel_id=1, source_target_pairs={{0,0},{1,128},{128,1},{129,129},{2,2},{3,130},{130,3},{131,131},{4... | collective-permute-start | bytes 589832 | tf_op jit(solution)/shard_map/ppermute | solution.py:281
  (12 other events, 155.8 us)
